TPU v7x, 32 devices: a whole 2x2x4 slice. The times are simulated.
32 devices in a mesh: row: 8 (over z, x), col: 4 (over y, core).
Axes of the slice: x: 2, y: 2, z: 4, core: 2. Of those that a mesh axis runs over, the one named last changes fastest.
Arguments:
- points: float32 [3, 4096], P(None, ('row', 'col')), may hold values from 0 to 10, as said below
- weights: float32 [4096], P(('row', 'col')), may hold values from 0.5 to 4
- far_blocks: int32 [8, 8], P('row', 'col'), may hold values from 0 to 7, as said below
- row_pivots: int32 [8, 8, 2, 64], P('row', 'col'), may hold values from 0 to 511
- col_pivots: int32 [8, 8, 2, 64], P('row', 'col'), may hold values from 0 to 511
Outputs:
- factors_v: bfloat16 [8, 1024, 512], P('row', 'col')
- basis_q: bfloat16 [8, 1024, 512], P('row', None, 'col')
- tri_factor: float32 [8, 1024, 1024], P('row')
Inputs may be any that keep to these rules, and one draw needn't show every extreme that they name: `points`: the panels of cluster c lie in the unit box whose lowest corner is 3 * (c % 4, (c // 4) % 4, c // 16). `far_blocks`: for every slot, the partners of the 8 clusters form a single cycle through all clusters: no cluster is its own partner, and each cluster is the partner of exactly one cluster in each slot.
All inputs are finite; a program needn't handle non-finite values.
Results may differ from a plain program's by a relative error of at most 0.007.
The roundings to bfloat16 on the way count: a program that leaves them out, or rounds other values in their place, can miss the bound.
Values may be sent and summed in bfloat16 or wider, within the bound.
No kernel may reach another device: no remote copies, remote signals or barrier semaphores. Data moves between devices by JAX's collectives and lax.ppermute only.
A program may use at most 128 MiB of HBM per device.

v0:
```python
import jax
import jax.numpy as jnp
from jax import lax
from jax.sharding import PartitionSpec as P

M = 512


wave_number = 8.0


def helmholtz_kernel(sources, targets):
    delta_x = sources[0][:, None] - targets[0][None, :]
    delta_y = sources[1][:, None] - targets[1][None, :]
    delta_z = sources[2][:, None] - targets[2][None, :]
    distance = jnp.sqrt(delta_x * delta_x + delta_y * delta_y + delta_z * delta_z)
    return sources[3][:, None] * targets[3][None, :] * jnp.cos(wave_number * distance) / distance


def solve_lower(lower_factor, rhs, transposed):
    return lax.linalg.triangular_solve(
        lower_factor, rhs, left_side=True, lower=True, transpose_a=transposed
    )


def cross_block(own_points, partner_points, row_piv, col_piv):
    rank = row_piv.shape[1]
    left_list = []
    right_list = []
    for counter in range(row_piv.shape[0]):
        own_pivot = jnp.take(own_points, row_piv[counter], axis=1)
        far_pivot = jnp.take(partner_points, col_piv[counter], axis=1)
        col_panel = helmholtz_kernel(far_pivot, own_points)
        row_panel = helmholtz_kernel(own_pivot, partner_points)
        for left_old, right_old in zip(left_list, right_list):
            col_panel = col_panel - jnp.dot(
                jnp.take(right_old, col_piv[counter], axis=1).T,
                left_old,
                preferred_element_type=jnp.float32,
            )
            row_panel = row_panel - jnp.dot(
                jnp.take(left_old, row_piv[counter], axis=1).T,
                right_old,
                preferred_element_type=jnp.float32,
            )
        pivot_t = jnp.take(col_panel, row_piv[counter], axis=1)
        normal = jnp.dot(
            pivot_t, pivot_t.T, precision=lax.Precision.HIGHEST, preferred_element_type=jnp.float32
        )
        shift = jnp.sum(pivot_t * pivot_t) / rank + 1e-06
        normal = normal + shift * jnp.eye(rank, dtype=jnp.float32)
        lower_factor = jnp.linalg.cholesky(normal)
        coupling = solve_lower(lower_factor, solve_lower(lower_factor, pivot_t, False), True)
        right_new = jnp.dot(
            coupling, row_panel, precision=lax.Precision.HIGHEST, preferred_element_type=jnp.float32
        )
        left_list.append(col_panel.astype(jnp.bfloat16))
        right_list.append(right_new.astype(jnp.bfloat16))
    return (jnp.concatenate(left_list, 0), jnp.concatenate(right_list, 0))


def per_device(points, weights, far_blocks, row_pivots, col_pivots):
    local_data = jnp.concatenate([points, weights[None, :]], 0)
    cluster_size = points.shape[1] * lax.axis_size("col")
    panel_data = lax.all_gather(local_data, ("row", "col"), axis=1, tiled=True)
    cluster = lax.axis_index("row")
    own_points = lax.dynamic_slice_in_dim(panel_data, cluster * cluster_size, cluster_size, 1)
    left_parts = []
    right_parts = []
    for slot in range(far_blocks.shape[1]):
        partner = far_blocks[0, slot]
        partner_points = lax.dynamic_slice_in_dim(
            panel_data, partner * cluster_size, cluster_size, 1
        )
        left_block, right_block = cross_block(
            own_points, partner_points, row_pivots[0, slot], col_pivots[0, slot]
        )
        left_parts.append(left_block)
        right_parts.append(right_block)
    left_mine = jnp.concatenate(left_parts, 0)
    factors_v = jnp.concatenate(right_parts, 0)[None]
    ucat_rows = lax.all_to_all(left_mine, "col", split_axis=1, concat_axis=0, tiled=True)
    gram_part = lax.dot_general(
        ucat_rows, ucat_rows, (((1,), (1,)), ((), ())), preferred_element_type=jnp.float32
    )
    gram = lax.psum(gram_part, "col") / M
    columns = gram.shape[0]
    shift = jnp.trace(gram) / columns + 1e-06
    lower_factor = jnp.linalg.cholesky(gram + shift * jnp.eye(columns, dtype=jnp.float32))
    basis = solve_lower(lower_factor, ucat_rows.astype(jnp.float32), False)
    return (factors_v, basis.astype(jnp.bfloat16)[None], lower_factor[None])


def solution(mesh):
    return jax.shard_map(
        per_device,
        mesh=mesh,
        in_specs=(
            P(None, ("row", "col")),
            P(("row", "col")),
            P("row", "col"),
            P("row", "col", None, None),
            P("row", "col", None, None),
        ),
        out_specs=(P("row", "col", None), P("row", None, "col"), P("row", None, None)),
        check_vma=False,
    )
```

profile of v0, /device:TPU:0, one launch (start us, length us, event | category | flops | bytes accessed | tf_op | source)
XLA Modules:
  0.0 585.3 jit_solution(14517423435381799936)
XLA Ops:
  10.6 49.4 %all_gather.3 = f32[4,4096]{0,1:T(8,128)S(1)} all-gather(f32[4,128]{0,1:T(8,128)S(1)} %copy.83), channel_id=1, replica_groups=mesh['row'=8,'col'=4] {'row','col'}, dimensions={1}, use_global_device_ids=true | all-gather | bytes 67584 | tf_op jit(solution)/shard_map/all_gather | solution.py:65
  67.8 5.8 cholesky.673
  75.0 4.9 custom-call.89
  86.9 5.8 cholesky.651
  94.1 4.9 custom-call.85
  105.7 3.4 all-to-all-start
  112.3 5.8 cholesky.684
  119.5 4.9 custom-call.91
  128.0 5.8 cholesky.662
  135.3 2.7 fusion.209
  139.0 4.9 custom-call.87
  147.9 73.5 %all-reduce.3.cloned.1.call-done = f32[1024,1024]{0,1:T(8,128)} async-done(((f32[1024,1024]{0,1:T(8,128)}), f32[1024,1024]{0,1:T(8,128)}) %all-reduce.3.cloned.1.call-update) | async-done | bytes 4194320 | tf_op jit(solution)/shard_map/psum | solution.py:86
  221.4 2.9 select_reduce_fusion
  225.0 5.1 select_add_fusion
  230.1 5.5 copy.102
  235.6 4.5 fusion
  242.1 11.7 %cholesky.247 = f32[128,128]{1,0:T(8,128)S(1)} custom-call(f32[128,128]{1,0:T(8,128)S(1)} %cholesky.693), custom_call_target="Cholesky" | custom-call | tf_op jit(solution)/shard_map/jit(cholesky)/cholesky | solution.py:89
  253.9 9.8 %custom-call.70 = f32[1,128,128]{1,2,0:T(8,128)S(1)} custom-call(f32[1,128,128]{2,1,0:T(8,128)S(1)} %get-tuple-element.143), custom_call_target="InvertDiagBlocksLowerTriangular" | custom-call | tf_op jit(solution)/shard_map/jit(cholesky)/cholesky | solution.py:89
  267.0 11.7 %cholesky.270 = f32[128,128]{1,0:T(8,128)S(1)} custom-call(f32[128,128]{1,0:T(8,128)S(1)} %cholesky.697), custom_call_target="Cholesky" | custom-call | tf_op jit(solution)/shard_map/jit(cholesky)/cholesky | solution.py:89
  279.1 9.8 %custom-call.71 = f32[1,128,128]{1,2,0:T(8,128)S(1)} custom-call(f32[1,128,128]{2,1,0:T(8,128)S(1)} %get-tuple-element.141), custom_call_target="InvertDiagBlocksLowerTriangular" | custom-call | tf_op jit(solution)/shard_map/jit(cholesky)/cholesky | solution.py:89
  292.0 2.4 convolution_subtract_fusion.1
  294.4 11.7 %cholesky.493 = f32[128,128]{1,0:T(8,128)S(1)} custom-call(f32[128,128]{1,0:T(8,128)S(1)} %cholesky.702), custom_call_target="Cholesky" | custom-call | tf_op jit(solution)/shard_map/jit(cholesky)/cholesky | solution.py:89
  306.9 9.8 %custom-call.72 = f32[1,128,128]{1,2,0:T(8,128)S(1)} custom-call(f32[1,128,128]{2,1,0:T(8,128)S(1)} %get-tuple-element.139), custom_call_target="InvertDiagBlocksLowerTriangular" | custom-call | tf_op jit(solution)/shard_map/jit(cholesky)/cholesky | solution.py:89
  318.0 3.5 convolution_subtract_fusion.2
  321.5 11.7 %cholesky.512 = f32[128,128]{1,0:T(8,128)S(1)} custom-call(f32[128,128]{1,0:T(8,128)S(1)} %cholesky.707), custom_call_target="Cholesky" | custom-call | tf_op jit(solution)/shard_map/jit(cholesky)/cholesky | solution.py:89
  334.0 9.8 %custom-call.73 = f32[1,128,128]{1,2,0:T(8,128)S(1)} custom-call(f32[1,128,128]{2,1,0:T(8,128)S(1)} %get-tuple-element.137), custom_call_target="InvertDiagBlocksLowerTriangular" | custom-call | tf_op jit(solution)/shard_map/jit(cholesky)/cholesky | solution.py:89
  344.9 3.1 convolution_subtract_fusion.3
  348.1 11.9 %cholesky.531 = f32[128,128]{1,0:T(8,128)S(1)} custom-call(f32[128,128]{1,0:T(8,128)S(1)} %cholesky.712), custom_call_target="Cholesky" | custom-call | tf_op jit(solution)/shard_map/jit(cholesky)/cholesky | solution.py:89
  360.7 9.8 %custom-call.74 = f32[1,128,128]{1,2,0:T(8,128)S(1)} custom-call(f32[1,128,128]{2,1,0:T(8,128)S(1)} %get-tuple-element.135), custom_call_target="InvertDiagBlocksLowerTriangular" | custom-call | tf_op jit(solution)/shard_map/jit(cholesky)/cholesky | solution.py:89
  371.7 3.1 convolution_subtract_fusion.4
  374.8 11.7 %cholesky.551 = f32[128,128]{1,0:T(8,128)S(1)} custom-call(f32[128,128]{1,0:T(8,128)S(1)} %cholesky.717), custom_call_target="Cholesky" | custom-call | tf_op jit(solution)/shard_map/jit(cholesky)/cholesky | solution.py:89
  387.3 9.8 %custom-call.75 = f32[1,128,128]{1,2,0:T(8,128)S(1)} custom-call(f32[1,128,128]{2,1,0:T(8,128)S(1)} %get-tuple-element.133), custom_call_target="InvertDiagBlocksLowerTriangular" | custom-call | tf_op jit(solution)/shard_map/jit(cholesky)/cholesky | solution.py:89
  398.1 2.9 convolution_subtract_fusion.5
  401.0 11.7 %cholesky.571 = f32[128,128]{1,0:T(8,128)S(1)} custom-call(f32[128,128]{1,0:T(8,128)S(1)} %cholesky.722), custom_call_target="Cholesky" | custom-call | tf_op jit(solution)/shard_map/jit(cholesky)/cholesky | solution.py:89
  413.4 9.8 %custom-call.76 = f32[1,128,128]{1,2,0:T(8,128)S(1)} custom-call(f32[1,128,128]{2,1,0:T(8,128)S(1)} %get-tuple-element.131), custom_call_target="InvertDiagBlocksLowerTriangular" | custom-call | tf_op jit(solution)/shard_map/jit(cholesky)/cholesky | solution.py:89
  426.3 11.7 %cholesky.589 = f32[128,128]{1,0:T(8,128)S(1)} custom-call(f32[128,128]{1,0:T(8,128)S(1)} %convolution_subtract_fusion.15), custom_call_target="Cholesky" | custom-call | tf_op jit(solution)/shard_map/jit(cholesky)/cholesky | solution.py:89
  449.1 6.8 %fusion.2 = (f32[1,1024,1024]{1,2,0:T(8,128)}, f32[1024,1024]{0,1:T(8,128)}) fusion(f32[1024,1024]{0,1:T(8,128)} %constant_dynamic-update-slice_fusion.30, pred[]{:T(512)S(6)} %cholesky.648), kind=kLoop, calls=%fused_computation.26 | loop fusion | flops 4194304 | bytes 12582913 | tf_op jit(solution)/shard_map/broadcast_in_dim | solution.py:91
  455.9 24.1 %while.1 = (s32[]{:T(128)}, f32[1024,1024]{0,1:T(8,128)}, s32[8,2]{0,1:T(2,128)S(1)}, f32[8,128,128]{2,1,0:T(8,128)S(1)}, s32[]{:T(128)}) while((s32[]{:T(128)}, f32[1024,1024]{0,1:T(8,128)}, s32[8,2]{0,1:T(2,128)S(1)}, f32[8,128,128]{2,1,0:T(8,128)S(1)}, s32[]{:T(128)}) %tuple.133), condition=%wide.while_cond, body=%wide.while_body.sunk | while | flops 2 | bytes 393329 | solution.py:21
  456.7 2.3 dynamic-slice.31
  459.7 2.3 dynamic-slice.31
  462.7 2.3 dynamic-slice.31
  465.7 2.3 dynamic-slice.31
  468.7 2.3 dynamic-slice.31
  471.7 2.3 dynamic-slice.31
  474.7 2.3 dynamic-slice.31
  477.7 2.2 dynamic-slice.31
  480.0 78.6 %custom-call.77 = f32[8,128,128]{1,2,0:T(8,128)S(1)} custom-call(f32[8,128,128]{2,1,0:T(8,128)S(1)} %get-tuple-element.16), custom_call_target="InvertDiagBlocksLowerTriangular" | custom-call | tf_op jit(solution)/shard_map/triangular_solve | solution.py:21
  571.7 5.3 copy.119
  (218 shorter events, 83.7 us)
Async XLA Ops:
  105.7 29.6 %all-to-all-start = ((bf16[256,4,128]{2,0,1:T(8,128)(2,1)}), bf16[256,4,128]{2,0,1:T(8,128)(2,1)S(1)}, u32[]{:S(2)}, u32[]{:S(2)}) async-start(bf16[256,4,128]{2,0,1:T(8,128)(2,1)} %copy_bitcast_fusion), calls=%async_computation | async-start | bytes 524288 | tf_op jit(solution)/shard_map/all_to_all | solution.py:82
  109.2 112.3 %all-reduce.3.cloned.1.call-start = ((), (), s32[]{:S(2)}) async-start(), calls=%async_computation.1 | async-start | bytes 8388608 | tf_op jit(solution)/shard_map/psum | solution.py:86
  240.0 2.0 copy-start.1
  290.0 2.0 copy-start
  577.3 0.7 copy-start.2
Sparse Core Ops, SparseCore 0:
  138.2 83.1 all-reduce.2
where the time goes:
time: 595 us; the launch traced here: 585 us
  other arithmetic  322 us (54%)
  waiting for transfers between devices  73.5 us (12%)
  local copies, waits for them, and re-layouts  60.7 us (10%)
  matrix products  51.2 us (9%)
  blocking collectives  49.4 us (8%)
  between operations  25 us (4%)
    another operation x31, other arithmetic, per_device(): jnp.linalg.cholesky(gram + shift * jnp.eye(columns, dtype=jnp.float32))  168 us
    another operation x10, other arithmetic, solve_lower(): lax.linalg.triangular_solve(lower_factor, rhs, left_side=True, lower=True...  101 us
    psum x1, waiting for transfers between devices, per_device(): gram = lax.psum(gram_part, 'col') / M  73.5 us
    all_gather x1, blocking collectives, per_device(): panel_data = lax.all_gather(local_data, ('row', 'col'), axis=1, tiled=True)  49.4 us
    another operation x14, matrix products, per_device(): jnp.linalg.cholesky(gram + shift * jnp.eye(columns, dtype=jnp.float32))  26.2 us
    another operation x12, other arithmetic, cross_block(): lower_factor = jnp.linalg.cholesky(normal)  26.1 us
    another operation x40, local copies, waits for them, and re-layouts  23.6 us
    another operation x23, matrix products, solve_lower(): lax.linalg.triangular_solve(lower_factor, rhs, left_side=True, lower=True...  14.9 us
  transfers between devices with their start and end apart: 2, of which 1 were waited for; matrix products, arithmetic and copies ran while one was open for 6% of the time, Pallas kernels for 0%

commit v1 on v0

v1 whole, which is shorter than its diff:
```python
import functools
import math

import jax
import jax.numpy as jnp
from jax import lax
from jax.experimental import pallas as pl
from jax.experimental.pallas import tpu as pltpu
from jax.sharding import PartitionSpec as P

f32, bf16 = jnp.float32, jnp.bfloat16
LANES, SUB = 128, 8

WAVE_NUMBER = 8.0
SINE = [(-1.0) ** k * (2.0 * math.pi) ** (2 * k + 1) / math.factorial(2 * k + 1) for k in range(7)]
NN = (((1,), (0,)), ((), ()))
NT = (((1,), (1,)), ((), ()))
TN = (((0,), (0,)), ((), ()))


def dot(a, b, dims):
    return lax.dot_general(a, b, dims, preferred_element_type=f32)


def split(x):
    hi = x.astype(bf16)
    return hi, (x - hi.astype(f32)).astype(bf16)


def dot3(a, b, dims):
    ah, al = a if isinstance(a, tuple) else split(a)
    bh, bl = b if isinstance(b, tuple) else split(b)
    return dot(ah, bh, dims) + (dot(al, bh, dims) + dot(ah, bl, dims))


def row_bcast(x, j):
    return jnp.broadcast_to(x[j : j + 1, :], x.shape)


def eliminate(parts, groups):
    mats = parts[0]
    lane_shape = (SUB, LANES)
    sub = lax.broadcasted_iota(jnp.int32, lane_shape, 0)
    for g in range(groups):
        panel = {
            (i, t): jnp.broadcast_to(mats[i][:, SUB * g + t : SUB * g + t + 1], lane_shape)
            for i in range(g, groups)
            for t in range(SUB)
        }
        for j in range(SUB):
            scale = lax.rsqrt(row_bcast(panel[g, j], j))
            rows = [row_bcast(p[g], j) * scale for p in parts]
            ahead = {t: row_bcast(panel[g, t], j) * scale for t in range(j + 1, SUB)}
            for i in range(g, groups):
                m = panel[i, j] * scale
                if i == g:
                    m = jnp.where(sub > j, m, 0.0)
                for p, row in zip(parts, rows):
                    new = p[i] - m * row
                    p[i] = jnp.where(sub == j, row, new) if i == g else new
                for t, head in ahead.items():
                    panel[i, t] = panel[i, t] - m * head


def chol_kernel(ucat_ref, basis_ref, tri_ref, a_ref, y_ref, x_ref, pa_ref, pb_ref, sems):
    n, inner = ucat_ref.shape
    blk = LANES
    nb = n // blk
    col = lax.axis_index("col")
    own = pl.ds(pl.multiple_of(col * blk, blk), blk)
    y_ref[...] = ucat_ref[:, own].astype(f32)
    squares = jnp.zeros((SUB, inner), f32)
    for i in range(0, n, 128):
        rows = ucat_ref[i : i + 128, :]
        top = rows.astype(f32)
        squares = squares + jnp.sum((top * top).reshape(16, SUB, inner), axis=0)
        a_ref[i : i + 128, 0 : i + 128] = dot(rows, ucat_ref[0 : i + 128, :], NT) * (1.0 / inner)
    shift = jnp.sum(squares) * (1.0 / (inner * n)) + 1e-06
    eye = lax.broadcasted_iota(jnp.int32, (blk, blk), 0) == lax.broadcasted_iota(
        jnp.int32, (blk, blk), 1
    )

    def copy_out(b):
        strip = pl.ds(pl.multiple_of(b * blk, blk), blk)
        return pltpu.make_async_copy(a_ref.at[:, strip], tri_ref.at[0, :, strip], sems.at[b])

    def block(b, carry):
        here = pl.ds(pl.multiple_of(b * blk, blk), blk)
        d = a_ref[here, here] + jnp.where(eye, shift, 0.0)
        mats = [d[SUB * i : SUB * (i + 1), :] for i in range(blk // SUB)]
        ident = jnp.where(eye, 1.0, 0.0).astype(f32)
        inv = [ident[SUB * i : SUB * (i + 1), :] for i in range(blk // SUB)]
        eliminate([mats, inv], blk // SUB)
        factor_t = jnp.concatenate(mats, 0)
        upper = lax.broadcasted_iota(jnp.int32, (blk, blk), 0) <= lax.broadcasted_iota(
            jnp.int32, (blk, blk), 1
        )
        a_ref[here, here] = jnp.where(upper, factor_t, 0.0).T
        x = jnp.concatenate(inv, 0)
        xs = split(x)
        yb = dot3(xs, y_ref[here, :], NN)
        basis_ref[0, here, :] = yb.astype(bf16)
        ys = split(yb)

        for k in range(nb):

            @pl.when(b == k)
            def _():
                r0 = (k + 1) * blk
                strip = slice(k * blk, r0)
                if k:
                    a_ref[0 : k * blk, strip] = jnp.zeros((k * blk, blk), f32)
                if r0 < n:
                    low = dot3(a_ref[r0:, strip], xs, NT)
                    a_ref[r0:, strip] = low
                    lh, ll = split(low)
                    pa_ref[r0:, 0:blk] = lh
                    pa_ref[r0:, blk : 2 * blk] = ll
                    pa_ref[r0:, 2 * blk :] = lh
                    pb_ref[r0:, 0:blk] = lh
                    pb_ref[r0:, blk : 2 * blk] = lh
                    pb_ref[r0:, 2 * blk :] = ll
                    for c in range(r0, n, 2 * blk):
                        w = min(2 * blk, n - c)
                        a_ref[c:, c : c + w] -= dot(pa_ref[c:, :], pb_ref[c : c + w, :], NT)
                    y_ref[r0:, :] -= dot3((lh, ll), ys, NN)

        copy_out(b).start()
        return carry

    lax.fori_loop(0, nb, block, 0)
    for b in range(nb):
        copy_out(b).wait()


def factor(ucat, part):
    n, inner = ucat.shape
    vmem = pl.BlockSpec(memory_space=pltpu.VMEM)
    return pl.pallas_call(
        chol_kernel,
        out_shape=(
            jax.ShapeDtypeStruct((1, n, part), bf16),
            jax.ShapeDtypeStruct((1, n, n), f32),
        ),
        in_specs=[vmem],
        out_specs=(vmem, pl.BlockSpec(memory_space=pl.ANY)),
        scratch_shapes=[
            pltpu.VMEM((n, n), f32),
            pltpu.VMEM((n, part), f32),
            pltpu.VMEM((LANES, LANES), f32),
            pltpu.VMEM((n, 3 * LANES), bf16),
            pltpu.VMEM((n, 3 * LANES), bf16),
            pltpu.SemaphoreType.DMA((n // LANES,)),
        ],
        compiler_params=pltpu.CompilerParams(vmem_limit_bytes=48 << 20),
        name="factor",
    )(ucat)


def wave(a, b):
    dx, dy, dz = a[0] - b[0], a[1] - b[1], a[2] - b[2]
    square = dx * dx + dy * dy + dz * dz
    inverse = lax.rsqrt(square)
    turns = square * inverse * (WAVE_NUMBER / (2.0 * math.pi))
    rest = jnp.abs(turns - jnp.floor(turns + 0.5))
    x = 0.25 - rest
    xx = x * x
    poly = SINE[-1]
    for c in SINE[-2::-1]:
        poly = poly * xx + c
    return a[3] * b[3] * (poly * x * inverse)


def shifted_inverse(tops):
    rank = tops[0].shape[0]
    groups = rank // SUB
    r = lax.broadcasted_iota(jnp.int32, (rank, rank), 0)
    c = lax.broadcasted_iota(jnp.int32, (rank, rank), 1)
    all_rows = []
    for top in tops:
        s = split(top)
        shift = jnp.sum(top * top) * (1.0 / rank) + 1e-06
        normal = dot3(s, s, NT) + jnp.where(r == c, shift, 0.0)
        both = jnp.concatenate([normal, jnp.where(r == c, 1.0, 0.0).astype(f32)], 1)
        all_rows.append([both[SUB * i : SUB * (i + 1), :] for i in range(groups)])
    eliminate_many(all_rows, groups)
    return [jnp.concatenate(rows, 0)[:, rank:] for rows in all_rows]


def eliminate_many(mats, groups):
    for m in mats:
        eliminate([m], groups)


def cross_kernel(rank, far_ref, tile_ref, ucat_ref, right_ref, pts_ref, ij_ref, ijt_ref, c_ref, v_ref):
    devices = tile_ref.shape[0]
    cols = lax.axis_size("col")
    clusters = devices // cols
    size = cols * LANES
    local = far_ref.shape[1]
    slots = cols * local
    row, col = lax.axis_index("row"), lax.axis_index("col")

    for k in range(clusters):
        p = jnp.concatenate([tile_ref[k * cols + c, 0:4, :] for c in range(cols)], 1)
        hi, mid = split(p)
        lo = (p - hi.astype(f32) - mid.astype(f32)).astype(bf16)
        zero = jnp.zeros((4, size), bf16)
        pts_ref[16 * k : 16 * k + 16, :] = jnp.concatenate([hi, mid, lo, zero], 0)

    spots = lax.broadcasted_iota(jnp.int32, (size, LANES), 0)
    of = lax.broadcasted_iota(jnp.int32, (clusters, 16, LANES), 0)
    for c in range(cols):
        for s in range(local):
            found = []
            for kind in range(2):
                panel = tile_ref[row * cols + c, 4 + kind * local + s : 5 + kind * local + s, :].astype(jnp.int32)
                where = panel // size
                hot = jnp.where(spots == panel - where * size, 1.0, 0.0).astype(bf16)
                got = dot(pts_ref[...], hot, NN).reshape(clusters, 16, LANES)
                got = jnp.sum(jnp.where(of == where[None], got, 0.0), axis=0)
                found.append(got[0:4] + got[4:8] + got[8:12])
            at = 8 * (c * local + s)
            ij_ref[at : at + 8, :] = jnp.concatenate(found, 0)
    ijt_ref[...] = jnp.concatenate([ij_ref[...], jnp.zeros((LANES - 8 * slots, LANES), f32)], 0).T

    own = jnp.concatenate([tile_ref[row * cols + c, 0:4, :] for c in range(cols)], 1)
    own = [own[i : i + 1, :] for i in range(4)]

    def as_rows(slot, kind, k):
        at = 8 * slot + 4 * kind
        return [ij_ref[at + i : at + i + 1, k * rank : (k + 1) * rank] for i in range(4)]

    def as_columns(slot, kind, k):
        at = 8 * slot + 4 * kind
        return [ijt_ref[k * rank : (k + 1) * rank, at + i : at + i + 1] for i in range(4)]

    group = 4
    for first in range(0, slots, group):
        tops = [wave(as_columns(s, 1, 0), as_rows(s, 0, 0)) for s in range(first, first + group)]
        lowers = shifted_inverse(tops)
        for s, top, lower in zip(range(first, first + group), tops, lowers):
            low = split(lower)
            half = dot3(low, split(top), NN)
            coupling = dot3(low, split(half), TN)
            c_ref[s] = coupling
            v_t = dot3(split(wave(as_columns(s, 1, 1), as_rows(s, 0, 0))), split(coupling), NT).astype(bf16)
            v_ref[s] = v_t
            at = s * 2 * rank
            u0 = wave(as_columns(s, 1, 0), own).astype(bf16)
            ucat_ref[at : at + rank, :] = u0
            u1 = wave(as_columns(s, 1, 1), own) - dot(v_t, u0, NN)
            ucat_ref[at + rank : at + 2 * rank, :] = u1.astype(bf16)

    tops, rest = [], []
    for s in range(local):
        slot = col * local + s
        rows = ij_ref[pl.ds(pl.multiple_of(8 * slot, 8), 8), :]
        columns = rows.T
        i_row = [[rows[q : q + 1, k * rank : (k + 1) * rank] for q in range(4)] for k in range(2)]
        j_row = [[rows[4 + q : 5 + q, k * rank : (k + 1) * rank] for q in range(4)] for k in range(2)]
        i_col = [[columns[k * rank : (k + 1) * rank, q : q + 1] for q in range(4)] for k in range(2)]
        j_col = [[columns[k * rank : (k + 1) * rank, 4 + q : 5 + q] for q in range(4)] for k in range(2)]
        far = far_ref[0, s]
        there = jnp.concatenate([tile_ref[far * cols + c, 0:4, :] for c in range(cols)], 1)
        there = [there[q : q + 1, :] for q in range(4)]
        v0 = dot3(split(c_ref[slot]), split(wave(i_col[0], there)), NN).astype(bf16)
        at = s * 2 * rank
        right_ref[0, at : at + rank, :] = v0
        u_t = wave(i_col[1], j_row[0]).astype(bf16)
        row_panel = wave(i_col[1], there) - dot(u_t, v0, NN)
        u_i = wave(j_col[0], i_row[1]).astype(bf16)
        tops.append(wave(j_col[1], i_row[1]) - dot(v_ref[slot], u_i, NN))
        rest.append(row_panel)
    lowers = shifted_inverse(tops)
    for s in range(local):
        low = split(lowers[s])
        coupling = dot3(low, split(dot3(low, split(tops[s]), NN)), TN)
        at = (2 * s + 1) * rank
        right_ref[0, at : at + rank, :] = dot3(split(coupling), split(rest[s]), NN).astype(bf16)


def cross(far_blocks, tiles, rank, cols):
    local = far_blocks.shape[1]
    slots = cols * local
    clusters = tiles.shape[0] // cols
    size = cols * LANES
    vmem = pl.BlockSpec(memory_space=pltpu.VMEM)
    return pl.pallas_call(
        functools.partial(cross_kernel, rank),
        out_shape=(
            jax.ShapeDtypeStruct((slots * 2 * rank, size), bf16),
            jax.ShapeDtypeStruct((1, local * 2 * rank, size), bf16),
        ),
        in_specs=[pl.BlockSpec(memory_space=pltpu.SMEM), vmem],
        out_specs=(vmem, vmem),
        scratch_shapes=[
            pltpu.VMEM((16 * clusters, size), bf16),
            pltpu.VMEM((8 * slots, LANES), f32),
            pltpu.VMEM((LANES, LANES), f32),
            pltpu.VMEM((slots, rank, rank), f32),
            pltpu.VMEM((slots, rank, rank), bf16),
        ],
        compiler_params=pltpu.CompilerParams(vmem_limit_bytes=48 << 20),
        name="cross",
    )(far_blocks, tiles)


def per_device(points, weights, far_blocks, row_pivots, col_pivots):
    part = points.shape[1]
    cols = lax.axis_size("col")
    size = part * cols
    rank = row_pivots.shape[3]
    own = row_pivots[0] + lax.axis_index("row") * size
    far = col_pivots[0] + far_blocks[0][:, None, None] * size
    tile = jnp.concatenate(
        [points, weights[None], own.reshape(-1, part).astype(f32), far.reshape(-1, part).astype(f32)], 0
    )
    count = lax.axis_size("row") * cols
    tiles = lax.all_to_all(
        jnp.broadcast_to(tile[None], (count,) + tile.shape), ("row", "col"), split_axis=0, concat_axis=0, tiled=True
    )
    ucat, factors_v = cross(far_blocks, tiles, rank, cols)
    basis, lower = factor(ucat, part)
    return factors_v, basis, lower


def solution(mesh):
    return jax.shard_map(
        per_device,
        mesh=mesh,
        in_specs=(
            P(None, ("row", "col")),
            P(("row", "col")),
            P("row", "col"),
            P("row", "col", None, None),
            P("row", "col", None, None),
        ),
        out_specs=(P("row", "col", None), P("row", None, "col"), P("row", None, None)),
        check_vma=False,
    )
```

time: 595 us -> 86.8 us (0.15); the launches traced: 585 us -> 86.5 us
  other arithmetic: 322 us -> 2.12 us
  waiting for transfers between devices: 73.5 us -> 0 us
  Pallas kernels: 0 us -> 66.7 us
  local copies, waits for them, and re-layouts: 60.7 us -> 1.51 us
  matrix products: 51.2 us -> 0 us
  blocking collectives: 49.4 us -> 15.3 us
  between operations: 25 us -> 0.8 us
    another operation x53 -> x0, other arithmetic: 295 us -> none  [the longest x31 168 us: per_device(): jnp.linalg.cholesky(gram + shift * jnp.eye(columns, dtype=jnp.float32))]
    psum x1 -> x0, waiting for transfers between devices: 73.5 us -> none  [per_device(): gram = lax.psum(gram_part, 'col') / M]
    pallas_call x0 -> x2, Pallas kernels: none -> 66.7 us  [the longest x1 43.4 us: factor(): pl.pallas_call(chol_kernel, out_shape=(jax.ShapeDtypeStruct((1, n, part),...]
    all_gather x1 -> x0, blocking collectives: 49.4 us -> none  [per_device(): panel_data = lax.all_gather(local_data, ('row', 'col'), axis=1, tiled=True)]
    another operation x37 -> x0, matrix products: 41 us -> none  [the longest x14 26.2 us: per_device(): jnp.linalg.cholesky(gram + shift * jnp.eye(columns, dtype=jnp.float32))]
    another operation x67 -> x0, local copies, waits for them, and re-layouts: 29.2 us -> none
    all_to_all x0 -> x1, blocking collectives: none -> 15.3 us  [per_device(): lax.all_to_all(jnp.broadcast_to(tile[None], (count,) + tile.shape), ('row...]
    dot_general x13 -> x0, matrix products: 10.1 us -> none  [the longest x1 2.72 us: per_device(): lax.dot_general(ucat_rows, ucat_rows, (((1,), (1,)), ((), ())), preferred...]
  transfers between devices with their start and end apart: 2 -> 0, of which waited for: 1 -> 0; matrix products, arithmetic and copies ran while one was open for 6% -> 0% of each run, Pallas kernels for 0% -> 0%
where the time goes in v1:
time: 86.8 us; the launch traced here: 86.5 us
  Pallas kernels  66.7 us (77%)
  blocking collectives  15.3 us (18%)
  other arithmetic  2.12 us (2%)
  local copies, waits for them, and re-layouts  1.51 us (2%)
    pallas_call x1, Pallas kernels, factor(): pl.pallas_call(chol_kernel, out_shape=(jax.ShapeDtypeStruct((1, n, part),...  43.4 us
    pallas_call x1, Pallas kernels, cross(): pl.pallas_call(functools.partial(cross_kernel, rank), out_shape=(jax.Shap...  23.3 us
    all_to_all x1, blocking collectives, per_device(): lax.all_to_all(jnp.broadcast_to(tile[None], (count,) + tile.shape), ('row...  15.3 us

profile of v1, /device:TPU:0, one launch (start us, length us, event | category | flops | bytes accessed | tf_op | source)
XLA Modules:
  0.0 86.5 jit_solution(1701067605682474855)
XLA Ops:
  0.6 0.7 multiply_bitcast_fusion
  1.3 0.8 squeeze.4
  2.1 0.7 add_convert_fusion
  2.7 0.1 convert_element_type.10
  2.8 0.1 add_convert_fusion.1
  2.9 0.7 pad_maximum_fusion
  3.6 15.3 %all_to_all.5.tile_ref = f32[32,8,128]{2,1,0:T(8,128)S(1)} all-to-all(f32[32,8,128]{2,1,0:T(8,128)S(1)} %broadcast_in_dim.10), channel_id=1, replica_groups=mesh['row'=8,'col'=4] {'row','col'}, dimensions={0} | all-to-all | bytes 262144 | tf_op jit(solution)/shard_map/all_to_all | solution.py:320
  19.0 0.0 copy-start
  19.0 0.7 copy-done
  19.6 23.3 %cross.1 = (bf16[1024,512]{1,0:T(8,128)(2,1)S(1)}, bf16[1,256,512]{2,1,0:T(8,128)(2,1)}) custom-call(s32[1,2]{1,0:T(1,128)S(1)} %copy-done, f32[32,8,128]{2,1,0:T(8,128)S(1)} %all_to_all.5.tile_ref), custom_call_target="tpu_custom_call" | custom-call | tf_op jit(solution)/shard_map/cross/pallas_call | solution.py:289
  43.0 43.4 %factor.1 = (bf16[1,1024,128]{2,1,0:T(8,128)(2,1)}, f32[1,1024,1024]{2,1,0:T(8,128)}) custom-call(bf16[1024,512]{1,0:T(8,128)(2,1)S(1)} %get-tuple-element.8.ucat_ref), custom_call_target="tpu_custom_call" | custom-call | tf_op jit(solution)/shard_map/factor/pallas_call | solution.py:139
  (1 shorter events, 0.0 us)
Async XLA Ops:
  19.0 0.7 copy-start

commit v2 on v1

--- a/solution.py
+++ b/solution.py
@@ -12,6 +12,7 @@
 LANES, SUB = 128, 8
 
 WAVE_NUMBER = 8.0
+NEAR = 3
 SINE = [(-1.0) ** k * (2.0 * math.pi) ** (2 * k + 1) / math.factorial(2 * k + 1) for k in range(7)]
 NN = (((1,), (0,)), ((), ()))
 NT = (((1,), (1,)), ((), ()))
@@ -37,98 +38,213 @@
     return jnp.broadcast_to(x[j : j + 1, :], x.shape)
 
 
-def eliminate(parts, groups):
-    mats = parts[0]
-    lane_shape = (SUB, LANES)
-    sub = lax.broadcasted_iota(jnp.int32, lane_shape, 0)
+def lane_bcast(x, k):
+    return jnp.broadcast_to(x[:, k : k + 1], x.shape)
+
+
+def eliminate(many, groups, zero, near, between=None):
+    shape = many[0][0].shape
+    sub = lax.broadcasted_iota(jnp.int32, shape, 0)
+    lane = lax.broadcasted_iota(jnp.int32, shape, 1)
+    diagonals = [[lane_bcast(mats[0], t) + zero for t in range(SUB)] for mats in many]
     for g in range(groups):
-        panel = {
-            (i, t): jnp.broadcast_to(mats[i][:, SUB * g + t : SUB * g + t + 1], lane_shape)
-            for i in range(g, groups)
-            for t in range(SUB)
-        }
-        for j in range(SUB):
-            scale = lax.rsqrt(row_bcast(panel[g, j], j))
-            rows = [row_bcast(p[g], j) * scale for p in parts]
-            ahead = {t: row_bcast(panel[g, t], j) * scale for t in range(j + 1, SUB)}
-            for i in range(g, groups):
-                m = panel[i, j] * scale
-                if i == g:
-                    m = jnp.where(sub > j, m, 0.0)
-                for p, row in zip(parts, rows):
-                    new = p[i] - m * row
-                    p[i] = jnp.where(sub == j, row, new) if i == g else new
-                for t, head in ahead.items():
-                    panel[i, t] = panel[i, t] - m * head
-
-
-def chol_kernel(ucat_ref, basis_ref, tri_ref, a_ref, y_ref, x_ref, pa_ref, pb_ref, sems):
+        for which, mats in enumerate(many):
+            diag = diagonals[which]
+            more = g + 1 < groups
+            if more:
+                under = [lane_bcast(mats[g + 1], SUB * g + t) for t in range(SUB)]
+                under[0] = under[0] + zero
+                ahead = [lane_bcast(mats[g + 1], SUB * (g + 1) + t) for t in range(SUB)]
+            rows, heads, scale = [], [], None
+            for j in range(SUB):
+                c = diag[j]
+                root = lax.rsqrt(row_bcast(c, j))
+                inv = root * root
+                below = jnp.where(sub > j, c, 0.0)
+                head = {}
+                for t in range(j + 1, SUB):
+                    raw = row_bcast(c, t)
+                    head[t] = raw * inv
+                    diag[t] = diag[t] - ((below * raw) * inv if t == j + 1 else below * head[t])
+                row = row_bcast(mats[g], j) * jnp.where(lane == SUB * g + j, inv + inv, inv)
+                mats[g] = mats[g] - below * row
+                scale = root if j == 0 else jnp.where(sub == j, root, scale)
+                rows.append(row)
+                heads.append(head)
+                if more:
+                    c = under[j]
+                    scaled = c * inv
+                    for t in range(j + 1, SUB):
+                        under[t] = under[t] - c * head[t]
+                    for t in range(SUB):
+                        ahead[t] = ahead[t] - scaled * row_bcast(c, t)
+                    mats[g + 1] = mats[g + 1] - c * row
+            mats[g] = mats[g] * scale
+            if g + near + 1 < groups:
+                inside = (lane >= SUB * g) & (lane < SUB * (g + 1))
+                high, low = split(mats[g])
+                right = jnp.where(inside & (lane > SUB * g + sub), 0.0, mats[g])
+                right_high, right_low = split(right)
+                none = jnp.zeros_like(high)
+                product = dot(
+                    jnp.concatenate([high, high, low, none], 0),
+                    jnp.concatenate([right_high, right_low, right_high, none], 0),
+                    TN,
+                )
+                for i in range(g + near + 1, groups):
+                    mats[i] = jnp.where(inside, 0.0, mats[i]) - product[SUB * i : SUB * (i + 1), :]
+            for i in range(g + 2, min(groups, g + near + 1)):
+                p = [lane_bcast(mats[i], SUB * g + t) for t in range(SUB)]
+                for j in range(SUB):
+                    for t in range(j + 1, SUB):
+                        p[t] = p[t] - p[j] * heads[j][t]
+                    mats[i] = mats[i] - p[j] * rows[j]
+            if more:
+                diagonals[which] = ahead
+        if between:
+            between(g)
+
+
+def factors_of(mats, size):
+    both = jnp.concatenate(mats, 0)[:, :size]
+    r = lax.broadcasted_iota(jnp.int32, (size, size), 0)
+    c = lax.broadcasted_iota(jnp.int32, (size, size), 1)
+    root = jnp.sum(jnp.where(r == c, both, 0.0), axis=0, keepdims=True)
+    inv = lax.rsqrt(root * root)
+    return both, jnp.where(c <= r, both * (inv * inv), 0.0)
+
+
+def pair(x):
+    return jnp.concatenate(split(x), 1)
+
+
+def times(a, b):
+    high, low = b
+    k, n = high.shape
+    right = jnp.concatenate(
+        [jnp.concatenate([high, low], 1), jnp.concatenate([high, jnp.zeros_like(low)], 1)], 0
+    )
+    out = dot(a, right, NN)
+    return out[:, :n] + out[:, n:]
+
+
+def times_t(a, b):
+    high, low = b
+    n, k = high.shape
+    right = jnp.concatenate(
+        [jnp.concatenate([high, high], 1), jnp.concatenate([low, jnp.zeros_like(low)], 1)], 0
+    )
+    out = dot(a, right, NT)
+    return out[:, :n] + out[:, n:]
+
+
+def chol_kernel(ucat_ref, basis_ref, tri_ref, a_ref, o_ref, y_ref, d_ref, l_ref, x_ref, p_ref, sems):
     n, inner = ucat_ref.shape
     blk = LANES
     nb = n // blk
+    wide = 2 * blk
+    groups = blk // SUB
     col = lax.axis_index("col")
     own = pl.ds(pl.multiple_of(col * blk, blk), blk)
-    y_ref[...] = ucat_ref[:, own].astype(f32)
+    row_id = lax.broadcasted_iota(jnp.int32, (blk, blk), 0)
+    col_id = lax.broadcasted_iota(jnp.int32, (blk, blk), 1)
+    eye = row_id == col_id
+    tiles = [(slice(r, r + wide), slice(c, c + wide)) for c in range(0, n, wide) for r in range(c, n, wide)]
+
     squares = jnp.zeros((SUB, inner), f32)
-    for i in range(0, n, 128):
-        rows = ucat_ref[i : i + 128, :]
-        top = rows.astype(f32)
-        squares = squares + jnp.sum((top * top).reshape(16, SUB, inner), axis=0)
-        a_ref[i : i + 128, 0 : i + 128] = dot(rows, ucat_ref[0 : i + 128, :], NT) * (1.0 / inner)
+    for i in range(0, n, blk):
+        top = ucat_ref[i : i + blk, :].astype(f32)
+        squares = squares + jnp.sum((top * top).reshape(blk // SUB, SUB, inner), axis=0)
     shift = jnp.sum(squares) * (1.0 / (inner * n)) + 1e-06
-    eye = lax.broadcasted_iota(jnp.int32, (blk, blk), 0) == lax.broadcasted_iota(
-        jnp.int32, (blk, blk), 1
-    )
+    zero = jnp.zeros((SUB, LANES), f32) + shift * 0.0
+
+    def diagonal(d, steps):
+        d = d + jnp.where(eye, shift, 0.0)
+        mats = [d[SUB * i : SUB * (i + 1), :] for i in range(groups)]
+        steps = list(steps)
+        turns = [steps[len(steps) * g // groups : len(steps) * (g + 1) // groups] for g in range(groups)]
+
+        def between(g):
+            for step in turns[g]:
+                step()
+
+        eliminate([mats], groups, zero, NEAR, between)
+        both, inverse = factors_of(mats, blk)
+        return jnp.where(row_id <= col_id, both, 0.0).T, split(inverse)
+
+    def spread(low, xs, b):
+        nxt = jnp.minimum(b + 1, nb - 1)
+        under = pl.ds(pl.multiple_of(nxt * blk, blk), blk)
+        here = pl.ds(pl.multiple_of(b * blk, blk), blk)
+        below = split(times_t(pair(a_ref[under, here]), xs))
+        d_ref[...] = a_ref[under, under] - times_t(jnp.concatenate(below, 1), below)
+        l_ref[...] = low
+        x_ref[0] = xs[0]
+        x_ref[1] = xs[1]
 
     def copy_out(b):
         strip = pl.ds(pl.multiple_of(b * blk, blk), blk)
-        return pltpu.make_async_copy(a_ref.at[:, strip], tri_ref.at[0, :, strip], sems.at[b])
+        return pltpu.make_async_copy(o_ref.at[b], tri_ref.at[0, :, strip], sems.at[b])
+
+    y_ref[...] = ucat_ref[:, own].astype(f32)
+
+    def gram(rows, cols):
+        return dot(ucat_ref[rows, :], ucat_ref[cols, :], NT) * (1.0 / inner)
+
+    def gram_step(rows, cols):
+        a_ref[rows, cols] = gram(rows, cols)
+
+    corner = slice(0, blk)
+    low, xs = diagonal(gram(corner, corner), [functools.partial(gram_step, *t) for t in tiles])
+    spread(low, xs, 0)
 
     def block(b, carry):
-        here = pl.ds(pl.multiple_of(b * blk, blk), blk)
-        d = a_ref[here, here] + jnp.where(eye, shift, 0.0)
-        mats = [d[SUB * i : SUB * (i + 1), :] for i in range(blk // SUB)]
-        ident = jnp.where(eye, 1.0, 0.0).astype(f32)
-        inv = [ident[SUB * i : SUB * (i + 1), :] for i in range(blk // SUB)]
-        eliminate([mats, inv], blk // SUB)
-        factor_t = jnp.concatenate(mats, 0)
-        upper = lax.broadcasted_iota(jnp.int32, (blk, blk), 0) <= lax.broadcasted_iota(
-            jnp.int32, (blk, blk), 1
-        )
-        a_ref[here, here] = jnp.where(upper, factor_t, 0.0).T
-        x = jnp.concatenate(inv, 0)
-        xs = split(x)
-        yb = dot3(xs, y_ref[here, :], NN)
-        basis_ref[0, here, :] = yb.astype(bf16)
-        ys = split(yb)
-
-        for k in range(nb):
-
-            @pl.when(b == k)
-            def _():
-                r0 = (k + 1) * blk
-                strip = slice(k * blk, r0)
-                if k:
-                    a_ref[0 : k * blk, strip] = jnp.zeros((k * blk, blk), f32)
-                if r0 < n:
-                    low = dot3(a_ref[r0:, strip], xs, NT)
-                    a_ref[r0:, strip] = low
-                    lh, ll = split(low)
-                    pa_ref[r0:, 0:blk] = lh
-                    pa_ref[r0:, blk : 2 * blk] = ll
-                    pa_ref[r0:, 2 * blk :] = lh
-                    pb_ref[r0:, 0:blk] = lh
-                    pb_ref[r0:, blk : 2 * blk] = lh
-                    pb_ref[r0:, 2 * blk :] = ll
-                    for c in range(r0, n, 2 * blk):
-                        w = min(2 * blk, n - c)
-                        a_ref[c:, c : c + w] -= dot(pa_ref[c:, :], pb_ref[c : c + w, :], NT)
-                    y_ref[r0:, :] -= dot3((lh, ll), ys, NN)
-
-        copy_out(b).start()
+        done = b - 1
+        at = pl.ds(pl.multiple_of(done * blk, blk), blk)
+        xs_old = (x_ref[0], x_ref[1])
+        first = b * blk
+        later = {}
+
+        def solve_rows():
+            yb = times(jnp.concatenate(xs_old, 1), split(y_ref[at, :]))
+            basis_ref[0, at, :] = yb.astype(bf16)
+            later["y"] = split(yb)
+
+        def panel(r):
+            rows = slice(r, r + wide)
+            p = times_t(pair(a_ref[rows, at]), xs_old)
+            ids = lax.broadcasted_iota(jnp.int32, (wide, blk), 0) + r
+            p = jnp.where(ids >= first, p, 0.0)
+            o_ref[done, rows, :] = p
+            p_ref[rows, :] = pair(p)
+
+        def trail(rows, cols):
+            left = p_ref[rows, :]
+            high, low = p_ref[cols, :blk], p_ref[cols, blk:]
+            left = jnp.concatenate([left, left[:, :blk]], 1)
+            a_ref[rows, cols] -= dot(left, jnp.concatenate([high, high, low], 1), NT)
+
+        def rest(r):
+            rows = slice(r, r + wide)
+            y_ref[rows, :] -= times(p_ref[rows, :], later["y"])
+
+        steps = [solve_rows]
+        steps += [functools.partial(panel, r) for r in range(0, n, wide)]
+        steps += [functools.partial(trail, *t) for t in tiles]
+        steps += [functools.partial(rest, r) for r in range(0, n, wide)]
+        low, xs = diagonal(d_ref[...], steps)
+        o_ref[done, at, :] = l_ref[...]
+        copy_out(done).start()
+        spread(low, xs, b)
         return carry
 
-    lax.fori_loop(0, nb, block, 0)
+    lax.fori_loop(1, nb, block, 0)
+    last = slice(n - blk, n)
+    o_ref[nb - 1, 0 : n - blk, :] = jnp.zeros((n - blk, blk), f32)
+    o_ref[nb - 1, last, :] = l_ref[...]
+    copy_out(nb - 1).start()
+    xs = jnp.concatenate([x_ref[0], x_ref[1]], 1)
+    basis_ref[0, last, :] = times(xs, split(y_ref[last, :])).astype(bf16)
     for b in range(nb):
         copy_out(b).wait()
 
@@ -146,10 +262,12 @@
         out_specs=(vmem, pl.BlockSpec(memory_space=pl.ANY)),
         scratch_shapes=[
             pltpu.VMEM((n, n), f32),
+            pltpu.VMEM((n // LANES, n, LANES), f32),
             pltpu.VMEM((n, part), f32),
             pltpu.VMEM((LANES, LANES), f32),
-            pltpu.VMEM((n, 3 * LANES), bf16),
-            pltpu.VMEM((n, 3 * LANES), bf16),
+            pltpu.VMEM((LANES, LANES), f32),
+            pltpu.VMEM((2, LANES, LANES), bf16),
+            pltpu.VMEM((n, 2 * LANES), bf16),
             pltpu.SemaphoreType.DMA((n // LANES,)),
         ],
         compiler_params=pltpu.CompilerParams(vmem_limit_bytes=48 << 20),
@@ -181,15 +299,10 @@
         s = split(top)
         shift = jnp.sum(top * top) * (1.0 / rank) + 1e-06
         normal = dot3(s, s, NT) + jnp.where(r == c, shift, 0.0)
-        both = jnp.concatenate([normal, jnp.where(r == c, 1.0, 0.0).astype(f32)], 1)
-        all_rows.append([both[SUB * i : SUB * (i + 1), :] for i in range(groups)])
-    eliminate_many(all_rows, groups)
-    return [jnp.concatenate(rows, 0)[:, rank:] for rows in all_rows]
-
-
-def eliminate_many(mats, groups):
-    for m in mats:
-        eliminate([m], groups)
+        normal = jnp.concatenate([normal, jnp.zeros((rank, LANES - rank), f32)], 1)
+        all_rows.append([normal[SUB * i : SUB * (i + 1), :] for i in range(groups)])
+    eliminate(all_rows, groups, jnp.zeros((SUB, LANES), f32) + jnp.max(tops[0]) * 0.0, groups)
+    return [factors_of(rows, rank)[1] for rows in all_rows]
 
 
 def cross_kernel(rank, far_ref, tile_ref, ucat_ref, right_ref, pts_ref, ij_ref, ijt_ref, c_ref, v_ref):

time: 86.8 us -> 64 us (0.74)
  Pallas kernels: 66.7 us -> 44 us
    pallas_call x1, Pallas kernels: 43.4 us -> 27.6 us  [factor(): pl.pallas_call(chol_kernel, out_shape=(jax.ShapeDtypeStruct((1, n, part),...]
    pallas_call x1, Pallas kernels: 23.3 us -> 16.4 us  [cross(): pl.pallas_call(functools.partial(cross_kernel, rank), out_shape=(jax.Shap...]
where the time goes in v2:
time: 64 us; the launch traced here: 63.7 us
  Pallas kernels  44 us (69%)
  blocking collectives  15.3 us (24%)
  other arithmetic  2.12 us (3%)
  local copies, waits for them, and re-layouts  1.51 us (2%)
  between operations  0.8 us (1%)
    pallas_call x1, Pallas kernels, factor(): pl.pallas_call(chol_kernel, out_shape=(jax.ShapeDtypeStruct((1, n, part),...  27.6 us
    pallas_call x1, Pallas kernels, cross(): pl.pallas_call(functools.partial(cross_kernel, rank), out_shape=(jax.Shap...  16.4 us
    all_to_all x1, blocking collectives, per_device(): lax.all_to_all(jnp.broadcast_to(tile[None], (count,) + tile.shape), ('row...  15.3 us

profile of v2, /device:TPU:0, one launch (start us, length us, event | category | flops | bytes accessed | tf_op | source)
XLA Modules:
  0.0 63.7 jit_solution(1390895391354977329)
XLA Ops:
  0.6 0.7 %multiply_bitcast_fusion = s32[2]{0:T(128)S(1)} fusion(s32[1,2]{1,0:T(1,128)} %far_ref.1), kind=kLoop, calls=%fused_computation.3 | loop fusion | flops 2 | bytes 16 | tf_op jit(solution)/shard_map/mul | solution.py:428
  1.3 0.8 %squeeze.4 = s32[2,128]{1,0:T(2,128)S(1)} reshape(s32[1,2,2,64]{3,2,1,0:T(2,128)} %param.9) | data formatting | bytes 2048 | tf_op jit(solution)/shard_map/squeeze | solution.py:428
  2.1 0.7 %add_convert_fusion = f32[1,2,2,64]{3,2,1,0:T(2,128)S(1)} fusion(s32[1,2,2,64]{3,2,1,0:T(2,128)} %param.8, s32[]{:T(128)S(6)} %mul.14), kind=kLoop, calls=%fused_computation.1 | loop fusion | flops 512 | bytes 2052 | tf_op jit(solution)/shard_map/convert_element_type | solution.py:430
  2.7 0.1 convert_element_type.10
  2.8 0.1 add_convert_fusion.1
  2.9 0.7 %pad_maximum_fusion = f32[8,128]{1,0:T(8,128)S(1)} fusion(f32[2,128]{1,0:T(2,128)S(1)} %add_convert_fusion.1, f32[2,128]{1,0:T(2,128)S(1)} %convert_element_type.10, f32[1,128]{1,0:T(1,128)} %bitcast.3, f32[3,128]{1,0:T(4,128)} %param.5), kind=kLoop, calls=%fused_computation | loop fusion | flops 3072 | bytes 8192 | tf_op jit(solution)/shard_map/concatenate | solution.py:429
  3.6 15.3 %all_to_all.5.tile_ref = f32[32,8,128]{2,1,0:T(8,128)S(1)} all-to-all(f32[32,8,128]{2,1,0:T(8,128)S(1)} %broadcast_in_dim.10), channel_id=1, replica_groups=mesh['row'=8,'col'=4] {'row','col'}, dimensions={0} | all-to-all | bytes 262144 | tf_op jit(solution)/shard_map/all_to_all | solution.py:433
  19.0 0.0 copy-start
  19.0 0.7 %copy-done = s32[1,2]{1,0:T(1,128)S(1)} copy-done((s32[1,2]{1,0:T(1,128)S(1)}, s32[1,2]{1,0:T(1,128)}, u32[]{:S(2)}) %copy-start) | copy-done | bytes 32
  19.6 16.4 %cross.1 = (bf16[1024,512]{1,0:T(8,128)(2,1)S(1)}, bf16[1,256,512]{2,1,0:T(8,128)(2,1)}) custom-call(s32[1,2]{1,0:T(1,128)S(1)} %copy-done, f32[32,8,128]{2,1,0:T(8,128)S(1)} %all_to_all.5.tile_ref), custom_call_target="tpu_custom_call" | custom-call | tf_op jit(solution)/shard_map/cross/pallas_call | solution.py:402
  36.0 27.6 %factor.1 = (bf16[1,1024,128]{2,1,0:T(8,128)(2,1)}, f32[1,1024,1024]{2,1,0:T(8,128)}) custom-call(bf16[1024,512]{1,0:T(8,128)(2,1)S(1)} %get-tuple-element.8.ucat_ref), custom_call_target="tpu_custom_call" | custom-call | tf_op jit(solution)/shard_map/factor/pallas_call | solution.py:255
  (1 shorter events, 0.0 us)
Async XLA Ops:
  19.0 0.7 %copy-start = (s32[1,2]{1,0:T(1,128)S(1)}, s32[1,2]{1,0:T(1,128)}, u32[]{:S(2)}) copy-start(s32[1,2]{1,0:T(1,128)} %far_ref.1) | copy-start | bytes 28

commit v3 on v2

--- a/solution.py
+++ b/solution.py
@@ -13,7 +13,7 @@
 
 WAVE_NUMBER = 8.0
 NEAR = 3
-SINE = [(-1.0) ** k * (2.0 * math.pi) ** (2 * k + 1) / math.factorial(2 * k + 1) for k in range(7)]
+SINE = [6.283185273658022, -41.341677416633885, 81.60222657697675, -76.5748772418381, 39.71002372452099]
 NN = (((1,), (0,)), ((), ()))
 NT = (((1,), (1,)), ((), ()))
 TN = (((0,), (0,)), ((), ()))
@@ -38,23 +38,38 @@
     return jnp.broadcast_to(x[j : j + 1, :], x.shape)
 
 
-def lane_bcast(x, k):
-    return jnp.broadcast_to(x[:, k : k + 1], x.shape)
-
-
-def eliminate(many, groups, zero, near, between=None):
+def eliminate(many, groups, near, width=LANES, zero=None, between=None):
     shape = many[0][0].shape
     sub = lax.broadcasted_iota(jnp.int32, shape, 0)
     lane = lax.broadcasted_iota(jnp.int32, shape, 1)
-    diagonals = [[lane_bcast(mats[0], t) + zero for t in range(SUB)] for mats in many]
+    start, spot = lane // width * width, lane % width
+    look = zero is not None
+
+    def lane_bcast(x, k):
+        if width == LANES:
+            return jnp.broadcast_to(x[:, k : k + 1], x.shape)
+        return jnp.take_along_axis(x, start + k, axis=1, mode="promise_in_bounds")
+
+    diagonals = [[lane_bcast(mats[0], t) + zero for t in range(SUB)] if look else None for mats in many]
     for g in range(groups):
-        for which, mats in enumerate(many):
-            diag = diagonals[which]
-            more = g + 1 < groups
+        last = min(groups, g + near + 1)
+        more = look and g + 1 < groups
+        panels = [{} for _ in many]
+        aheads = [{} for _ in many]
+        for t in range(SUB):
+            for mats, panel in zip(many, panels):
+                for i in range(g + 1 if look else g, last):
+                    panel[i, t] = lane_bcast(mats[i], SUB * g + t)
+            for mats, ahead in zip(many, aheads):
+                if more:
+                    ahead[t] = lane_bcast(mats[g + 1], SUB * (g + 1) + t)
+        for which, (mats, panel, ahead) in enumerate(zip(many, panels, aheads)):
+            if look:
+                diag = diagonals[which]
+            else:
+                diag = [panel[g, t] for t in range(SUB)]
             if more:
-                under = [lane_bcast(mats[g + 1], SUB * g + t) for t in range(SUB)]
-                under[0] = under[0] + zero
-                ahead = [lane_bcast(mats[g + 1], SUB * (g + 1) + t) for t in range(SUB)]
+                panel[g + 1, 0] = panel[g + 1, 0] + zero
             rows, heads, scale = [], [], None
             for j in range(SUB):
                 c = diag[j]
@@ -66,21 +81,21 @@
                     raw = row_bcast(c, t)
                     head[t] = raw * inv
                     diag[t] = diag[t] - ((below * raw) * inv if t == j + 1 else below * head[t])
-                row = row_bcast(mats[g], j) * jnp.where(lane == SUB * g + j, inv + inv, inv)
+                row = row_bcast(mats[g], j) * jnp.where(spot == SUB * g + j, inv + inv, inv)
                 mats[g] = mats[g] - below * row
                 scale = root if j == 0 else jnp.where(sub == j, root, scale)
                 rows.append(row)
                 heads.append(head)
                 if more:
-                    c = under[j]
+                    c = panel[g + 1, j]
                     scaled = c * inv
                     for t in range(j + 1, SUB):
-                        under[t] = under[t] - c * head[t]
+                        panel[g + 1, t] = panel[g + 1, t] - c * head[t]
                     for t in range(SUB):
                         ahead[t] = ahead[t] - scaled * row_bcast(c, t)
                     mats[g + 1] = mats[g + 1] - c * row
             mats[g] = mats[g] * scale
-            if g + near + 1 < groups:
+            if last < groups:
                 inside = (lane >= SUB * g) & (lane < SUB * (g + 1))
                 high, low = split(mats[g])
                 right = jnp.where(inside & (lane > SUB * g + sub), 0.0, mats[g])
@@ -91,27 +106,29 @@
                     jnp.concatenate([right_high, right_low, right_high, none], 0),
                     TN,
                 )
-                for i in range(g + near + 1, groups):
+                for i in range(last, groups):
                     mats[i] = jnp.where(inside, 0.0, mats[i]) - product[SUB * i : SUB * (i + 1), :]
-            for i in range(g + 2, min(groups, g + near + 1)):
-                p = [lane_bcast(mats[i], SUB * g + t) for t in range(SUB)]
+            for i in range(g + 2 if look else g + 1, last):
                 for j in range(SUB):
                     for t in range(j + 1, SUB):
-                        p[t] = p[t] - p[j] * heads[j][t]
-                    mats[i] = mats[i] - p[j] * rows[j]
-            if more:
-                diagonals[which] = ahead
+                        panel[i, t] = panel[i, t] - panel[i, j] * heads[j][t]
+                    mats[i] = mats[i] - panel[i, j] * rows[j]
+            diagonals[which] = ahead
         if between:
             between(g)
 
 
-def factors_of(mats, size):
-    both = jnp.concatenate(mats, 0)[:, :size]
-    r = lax.broadcasted_iota(jnp.int32, (size, size), 0)
-    c = lax.broadcasted_iota(jnp.int32, (size, size), 1)
+def factors_of(mats, width=LANES):
+    both = jnp.concatenate(mats, 0)
+    r = lax.broadcasted_iota(jnp.int32, both.shape, 0)
+    c = lax.broadcasted_iota(jnp.int32, both.shape, 1) % width
     root = jnp.sum(jnp.where(r == c, both, 0.0), axis=0, keepdims=True)
     inv = lax.rsqrt(root * root)
     return both, jnp.where(c <= r, both * (inv * inv), 0.0)
+
+
+def in_turns(steps, count):
+    return [steps[len(steps) * g // count : len(steps) * (g + 1) // count] for g in range(count)]
 
 
 def pair(x):
@@ -161,15 +178,14 @@
     def diagonal(d, steps):
         d = d + jnp.where(eye, shift, 0.0)
         mats = [d[SUB * i : SUB * (i + 1), :] for i in range(groups)]
-        steps = list(steps)
-        turns = [steps[len(steps) * g // groups : len(steps) * (g + 1) // groups] for g in range(groups)]
+        turns = steps
 
         def between(g):
             for step in turns[g]:
                 step()
 
-        eliminate([mats], groups, zero, NEAR, between)
-        both, inverse = factors_of(mats, blk)
+        eliminate([mats], groups, NEAR, LANES, zero, between)
+        both, inverse = factors_of(mats)
         return jnp.where(row_id <= col_id, both, 0.0).T, split(inverse)
 
     def spread(low, xs, b):
@@ -195,7 +211,7 @@
         a_ref[rows, cols] = gram(rows, cols)
 
     corner = slice(0, blk)
-    low, xs = diagonal(gram(corner, corner), [functools.partial(gram_step, *t) for t in tiles])
+    low, xs = diagonal(gram(corner, corner), in_turns([functools.partial(gram_step, *t) for t in tiles], groups))
     spread(low, xs, 0)
 
     def block(b, carry):
@@ -228,10 +244,10 @@
             rows = slice(r, r + wide)
             y_ref[rows, :] -= times(p_ref[rows, :], later["y"])
 
-        steps = [solve_rows]
-        steps += [functools.partial(panel, r) for r in range(0, n, wide)]
-        steps += [functools.partial(trail, *t) for t in tiles]
-        steps += [functools.partial(rest, r) for r in range(0, n, wide)]
+        panels = [functools.partial(panel, r) for r in range(0, n, wide)]
+        trails = [functools.partial(trail, *t) for t in tiles]
+        rests = [functools.partial(rest, r) for r in range(0, n, wide)]
+        steps = in_turns(panels, 2) + [[solve_rows]] + in_turns(trails + rests, groups - 3)
         low, xs = diagonal(d_ref[...], steps)
         o_ref[done, at, :] = l_ref[...]
         copy_out(done).start()
@@ -280,32 +296,46 @@
     square = dx * dx + dy * dy + dz * dz
     inverse = lax.rsqrt(square)
     turns = square * inverse * (WAVE_NUMBER / (2.0 * math.pi))
-    rest = jnp.abs(turns - jnp.floor(turns + 0.5))
-    x = 0.25 - rest
+    x = 0.25 - jnp.abs(turns - lax.round(turns, lax.RoundingMethod.TO_NEAREST_EVEN))
     xx = x * x
     poly = SINE[-1]
     for c in SINE[-2::-1]:
         poly = poly * xx + c
-    return a[3] * b[3] * (poly * x * inverse)
-
-
-def shifted_inverse(tops):
+    return (a[3] * b[3]) * (poly * x * inverse)
+
+
+def apart(x, left):
+    none = jnp.zeros_like(x)
+    return jnp.concatenate([jnp.where(left, x, none), jnp.where(left, none, x)], 0)
+
+
+def shifted_inverse(tops, look, fillers):
     rank = tops[0].shape[0]
     groups = rank // SUB
-    r = lax.broadcasted_iota(jnp.int32, (rank, rank), 0)
-    c = lax.broadcasted_iota(jnp.int32, (rank, rank), 1)
-    all_rows = []
+    r = lax.broadcasted_iota(jnp.int32, tops[0].shape, 0)
+    c = lax.broadcasted_iota(jnp.int32, tops[0].shape, 1)
+    left = c < rank
+    mats = []
     for top in tops:
-        s = split(top)
-        shift = jnp.sum(top * top) * (1.0 / rank) + 1e-06
-        normal = dot3(s, s, NT) + jnp.where(r == c, shift, 0.0)
-        normal = jnp.concatenate([normal, jnp.zeros((rank, LANES - rank), f32)], 1)
-        all_rows.append([normal[SUB * i : SUB * (i + 1), :] for i in range(groups)])
-    eliminate(all_rows, groups, jnp.zeros((SUB, LANES), f32) + jnp.max(tops[0]) * 0.0, groups)
-    return [factors_of(rows, rank)[1] for rows in all_rows]
-
-
-def cross_kernel(rank, far_ref, tile_ref, ucat_ref, right_ref, pts_ref, ij_ref, ijt_ref, c_ref, v_ref):
+        normal = times_t(pair(top), split(apart(top, left)))
+        squares = jnp.sum(top * top, axis=0, keepdims=True)
+        first = lax.broadcasted_iota(jnp.int32, squares.shape, 1) < rank
+        shift = [jnp.sum(jnp.where(first == side, squares, 0.0), axis=1, keepdims=True) for side in (True, False)]
+        shift = jnp.where(first, shift[0], shift[1]) * (1.0 / rank) + 1e-06
+        normal = normal + jnp.where(r == c % rank, shift, 0.0)
+        mats.append([normal[SUB * i : SUB * (i + 1), :] for i in range(groups)])
+    zero = jnp.zeros((SUB, LANES), f32) + jnp.max(tops[0]) * 0.0 if look else None
+    turns = in_turns(fillers, groups)
+
+    def between(g):
+        for step in turns[g]:
+            step()
+
+    eliminate(mats, groups, groups, rank, zero, between)
+    return [factors_of(rows, rank)[1] for rows in mats]
+
+
+def cross_kernel(rank, far_ref, tile_ref, ucat_ref, right_ref, pts_ref, ij_ref, ijt_ref, low_ref, half_ref, v_ref, panel_ref):
     devices = tile_ref.shape[0]
     cols = lax.axis_size("col")
     clusters = devices // cols
@@ -313,6 +343,7 @@
     local = far_ref.shape[1]
     slots = cols * local
     row, col = lax.axis_index("row"), lax.axis_index("col")
+    left = lax.broadcasted_iota(jnp.int32, (rank, LANES), 1) < rank
 
     for k in range(clusters):
         p = jnp.concatenate([tile_ref[k * cols + c, 0:4, :] for c in range(cols)], 1)
@@ -337,60 +368,104 @@
             ij_ref[at : at + 8, :] = jnp.concatenate(found, 0)
     ijt_ref[...] = jnp.concatenate([ij_ref[...], jnp.zeros((LANES - 8 * slots, LANES), f32)], 0).T
 
-    own = jnp.concatenate([tile_ref[row * cols + c, 0:4, :] for c in range(cols)], 1)
-    own = [own[i : i + 1, :] for i in range(4)]
-
-    def as_rows(slot, kind, k):
-        at = 8 * slot + 4 * kind
-        return [ij_ref[at + i : at + i + 1, k * rank : (k + 1) * rank] for i in range(4)]
-
-    def as_columns(slot, kind, k):
-        at = 8 * slot + 4 * kind
-        return [ijt_ref[k * rank : (k + 1) * rank, at + i : at + i + 1] for i in range(4)]
-
-    group = 4
-    for first in range(0, slots, group):
-        tops = [wave(as_columns(s, 1, 0), as_rows(s, 0, 0)) for s in range(first, first + group)]
-        lowers = shifted_inverse(tops)
-        for s, top, lower in zip(range(first, first + group), tops, lowers):
-            low = split(lower)
-            half = dot3(low, split(top), NN)
-            coupling = dot3(low, split(half), TN)
-            c_ref[s] = coupling
-            v_t = dot3(split(wave(as_columns(s, 1, 1), as_rows(s, 0, 0))), split(coupling), NT).astype(bf16)
-            v_ref[s] = v_t
-            at = s * 2 * rank
-            u0 = wave(as_columns(s, 1, 0), own).astype(bf16)
-            ucat_ref[at : at + rank, :] = u0
-            u1 = wave(as_columns(s, 1, 1), own) - dot(v_t, u0, NN)
-            ucat_ref[at + rank : at + 2 * rank, :] = u1.astype(bf16)
-
-    tops, rest = [], []
-    for s in range(local):
-        slot = col * local + s
-        rows = ij_ref[pl.ds(pl.multiple_of(8 * slot, 8), 8), :]
-        columns = rows.T
-        i_row = [[rows[q : q + 1, k * rank : (k + 1) * rank] for q in range(4)] for k in range(2)]
-        j_row = [[rows[4 + q : 5 + q, k * rank : (k + 1) * rank] for q in range(4)] for k in range(2)]
-        i_col = [[columns[k * rank : (k + 1) * rank, q : q + 1] for q in range(4)] for k in range(2)]
-        j_col = [[columns[k * rank : (k + 1) * rank, 4 + q : 5 + q] for q in range(4)] for k in range(2)]
-        far = far_ref[0, s]
-        there = jnp.concatenate([tile_ref[far * cols + c, 0:4, :] for c in range(cols)], 1)
-        there = [there[q : q + 1, :] for q in range(4)]
-        v0 = dot3(split(c_ref[slot]), split(wave(i_col[0], there)), NN).astype(bf16)
-        at = s * 2 * rank
-        right_ref[0, at : at + rank, :] = v0
-        u_t = wave(i_col[1], j_row[0]).astype(bf16)
-        row_panel = wave(i_col[1], there) - dot(u_t, v0, NN)
-        u_i = wave(j_col[0], i_row[1]).astype(bf16)
-        tops.append(wave(j_col[1], i_row[1]) - dot(v_ref[slot], u_i, NN))
-        rest.append(row_panel)
-    lowers = shifted_inverse(tops)
-    for s in range(local):
-        low = split(lowers[s])
-        coupling = dot3(low, split(dot3(low, split(tops[s]), NN)), TN)
-        at = (2 * s + 1) * rank
-        right_ref[0, at : at + rank, :] = dot3(split(coupling), split(rest[s]), NN).astype(bf16)
+    def points_of(tile):
+        both = jnp.concatenate([tile_ref[tile * cols + c, 0:4, :] for c in range(cols)], 1)
+        return [both[i : i + 1, :] for i in range(4)]
+
+    def columns(source, at, k):
+        part = source[k * rank : (k + 1) * rank, :]
+        return [jnp.broadcast_to(part[:, at + i : at + i + 1], (rank, LANES)) for i in range(4)]
+
+    def both_rows(a, b, k):
+        first = lax.broadcasted_iota(jnp.int32, (4, LANES), 1) < rank
+        a, b = (b, a) if k else (a, b)
+        other = pltpu.roll(b, rank, 1)
+        got = jnp.where(first, other, a) if k else jnp.where(first, a, other)
+        return [got[i : i + 1, :] for i in range(4)]
+
+    def both_columns(a, b):
+        return [jnp.where(left, x, y) for x, y in zip(a, b)]
+
+    def against(column, points):
+        wide = [jnp.concatenate([x] * cols, 1) for x in column]
+        return wave(wide, points)
+
+    own = points_of(row)
+
+    pairs = []
+    for s in range(0, slots, 2):
+        rows_i = [ij_ref[8 * (s + h) : 8 * (s + h) + 4, :] for h in range(2)]
+        j_cols = [[columns(ijt_ref, 8 * (s + h) + 4, k) for h in range(2)] for k in range(2)]
+        i_rows = both_rows(rows_i[0], rows_i[1], 0)
+        pairs.append([s, wave(both_columns(*j_cols[0]), i_rows), wave(both_columns(*j_cols[1]), i_rows), j_cols])
+
+    mine = []
+    for s in range(0, local, 2):
+        which = (col * local + s) // 2
+        rows = [ij_ref[pl.ds(pl.multiple_of(8 * (2 * which + h), 8), 8), :] for h in range(2)]
+        flat = [r.T for r in rows]
+        i_col = [[columns(flat[h], 0, k) for h in range(2)] for k in range(2)]
+        j_col = [[columns(flat[h], 4, k) for h in range(2)] for k in range(2)]
+        j_row = both_rows(rows[0][4:8], rows[1][4:8], 0)
+        i_row = both_rows(rows[0][0:4], rows[1][0:4], 1)
+        there = [points_of(far_ref[0, s + h]) for h in range(2)]
+        mine.append((s, which, i_col, j_col, j_row, i_row, there))
+
+    def left_factor(s, h, j_cols):
+        at = (s + h) * 2 * rank
+        ucat_ref[at : at + rank, :] = against(j_cols[0][h], own).astype(bf16)
+
+    def row_panel(s, k, h, column, there):
+        panel_ref[s // 2, k, h * rank : (h + 1) * rank, :] = against(column, there)
+
+    def next_left_factor(s, j_cols):
+        u0 = [ucat_ref[(s + h) * 2 * rank : (s + h) * 2 * rank + rank, :] for h in range(2)]
+        product = dot(apart(v_ref[s // 2], left), jnp.concatenate(u0, 0), NN)
+        for h in range(2):
+            at = (s + h) * 2 * rank + rank
+            u1 = against(j_cols[1][h], own) - product[h * rank : (h + 1) * rank]
+            ucat_ref[at : at + rank, :] = u1.astype(bf16)
+
+    fillers = [functools.partial(left_factor, p[0], h, p[3]) for p in pairs for h in range(2)]
+    for s, _, i_col, _, _, _, there in mine:
+        fillers += [
+            functools.partial(row_panel, s, k, h, i_col[k][h], there[h]) for k in range(2) for h in range(2)
+        ]
+    lowers = shifted_inverse([p[1] for p in pairs], False, fillers)
+    for (s, top, mixed, _), low in zip(pairs, lowers):
+        half = times(pair(low), split(apart(top, left)))
+        low_ref[s // 2] = low
+        half_ref[s // 2] = half
+        v_t = times_t(pair(mixed), split(apart(half, left)))
+        v_ref[s // 2] = times(pair(v_t), split(apart(low, left))).astype(bf16)
+
+    square = lax.broadcasted_iota(jnp.int32, (LANES, LANES), 0) < rank
+    same = square == (lax.broadcasted_iota(jnp.int32, (LANES, LANES), 1) < rank)
+
+    def couple(low, half, panel):
+        coupling = jnp.where(same, dot3(split(low), split(half), TN), 0.0)
+        high, low = split(coupling)
+        panel_high, panel_low = split(panel)
+        both = jnp.concatenate([high, low], 1)
+        return dot(both, jnp.concatenate([panel_high, panel_high], 0), NN) + dot(high, panel_low, NN)
+
+    fillers = [functools.partial(next_left_factor, p[0], p[3]) for p in pairs]
+    for s, which, i_col, j_col, j_row, i_row, there in mine:
+        top = wave(both_columns(*j_col[1]), i_row)
+        u_i = wave(both_columns(*j_col[0]), i_row).astype(bf16)
+        top = top - dot(v_ref[which], apart(u_i, left), NN)
+        v0 = couple(low_ref[which], half_ref[which], panel_ref[s // 2, 0]).astype(bf16)
+        u_t = wave(both_columns(*i_col[1]), j_row).astype(bf16)
+        rest = panel_ref[s // 2, 1] - dot(apart(u_t, left), v0, NN)
+        low = shifted_inverse([top], True, fillers[:len(pairs) - 1])[0]
+        fillers = fillers[len(pairs) - 1:]
+        v1 = couple(low, times(pair(low), split(apart(top, left))), rest).astype(bf16)
+        for h in range(2):
+            at = (s + h) * 2 * rank
+            right_ref[0, at : at + rank, :] = v0[h * rank : (h + 1) * rank]
+            right_ref[0, at + rank : at + 2 * rank, :] = v1[h * rank : (h + 1) * rank]
+    for step in fillers:
+        step()
 
 
 def cross(far_blocks, tiles, rank, cols):
@@ -411,28 +486,44 @@
             pltpu.VMEM((16 * clusters, size), bf16),
             pltpu.VMEM((8 * slots, LANES), f32),
             pltpu.VMEM((LANES, LANES), f32),
-            pltpu.VMEM((slots, rank, rank), f32),
-            pltpu.VMEM((slots, rank, rank), bf16),
+            pltpu.VMEM((slots // 2, rank, LANES), f32),
+            pltpu.VMEM((slots // 2, rank, LANES), f32),
+            pltpu.VMEM((slots // 2, rank, LANES), bf16),
+            pltpu.VMEM((local // 2, 2, 2 * rank, size), f32),
         ],
         compiler_params=pltpu.CompilerParams(vmem_limit_bytes=48 << 20),
         name="cross",
     )(far_blocks, tiles)
 
 
+def pack_kernel(size, far_ref, points_ref, weights_ref, row_ref, col_ref, out_ref):
+    local = far_ref.shape[1]
+    first = lax.axis_index("row") * size
+    own = [row_ref[0, s] + first for s in range(local)]
+    far = [col_ref[0, s] + far_ref[0, s] * size for s in range(local)]
+    flat = [jnp.concatenate([x[k : k + 1] for k in range(x.shape[0])], 1).astype(f32) for x in own + far]
+    tile = jnp.concatenate([points_ref[...], weights_ref[...]] + flat, 0)
+    out_ref[...] = jnp.broadcast_to(tile[None], out_ref.shape)
+
+
+def pack(far_blocks, points, weights, row_pivots, col_pivots, count, size):
+    vmem = pl.BlockSpec(memory_space=pltpu.VMEM)
+    return pl.pallas_call(
+        functools.partial(pack_kernel, size),
+        out_shape=jax.ShapeDtypeStruct((count, 4 + 2 * far_blocks.shape[1], points.shape[1]), f32),
+        in_specs=[pl.BlockSpec(memory_space=pltpu.SMEM), vmem, vmem, vmem, vmem],
+        out_specs=vmem,
+        name="pack",
+    )(far_blocks, points, weights[None], row_pivots, col_pivots)
+
+
 def per_device(points, weights, far_blocks, row_pivots, col_pivots):
     part = points.shape[1]
     cols = lax.axis_size("col")
-    size = part * cols
     rank = row_pivots.shape[3]
-    own = row_pivots[0] + lax.axis_index("row") * size
-    far = col_pivots[0] + far_blocks[0][:, None, None] * size
-    tile = jnp.concatenate(
-        [points, weights[None], own.reshape(-1, part).astype(f32), far.reshape(-1, part).astype(f32)], 0
-    )
     count = lax.axis_size("row") * cols
-    tiles = lax.all_to_all(
-        jnp.broadcast_to(tile[None], (count,) + tile.shape), ("row", "col"), split_axis=0, concat_axis=0, tiled=True
-    )
+    tiles = pack(far_blocks, points, weights, row_pivots, col_pivots, count, part * cols)
+    tiles = lax.all_to_all(tiles, ("row", "col"), split_axis=0, concat_axis=0, tiled=True)
     ucat, factors_v = cross(far_blocks, tiles, rank, cols)
     basis, lower = factor(ucat, part)
     return factors_v, basis, lower

time: 64 us -> 56.1 us (0.88)
  Pallas kernels: 44 us -> 39 us
  other arithmetic: 2.12 us -> 0 us
  local copies, waits for them, and re-layouts: 1.51 us -> 0.66 us
    pallas_call x1, Pallas kernels: 16.4 us -> 10.6 us  [cross(): pl.pallas_call(functools.partial(cross_kernel, rank), out_shape=(jax.Shap...]
    pallas_call x0 -> x1, Pallas kernels: none -> 1.55 us  [pack(): pl.pallas_call(functools.partial(pack_kernel, size), out_shape=jax.ShapeD...]
    pallas_call x1, Pallas kernels: 27.6 us -> 26.8 us  [factor(): pl.pallas_call(chol_kernel, out_shape=(jax.ShapeDtypeStruct((1, n, part),...]
    squeeze x1 -> x0, local copies, waits for them, and re-layouts: 0.76 us -> none  [per_device(): far = col_pivots[0] + far_blocks[0][:, None, None] * size]
    convert_element_type x2 -> x0, other arithmetic: 0.76 us -> none  [the longest x1 0.68 us: per_device(): own.reshape(-1, part).astype(f32)]
    concatenate x1 -> x0, other arithmetic: 0.71 us -> none  [per_device(): jnp.concatenate([points, weights[None], own.reshape(-1, part).astype(f32)...]
    mul x1 -> x0, other arithmetic: 0.66 us -> none  [per_device(): far = col_pivots[0] + far_blocks[0][:, None, None] * size]
where the time goes in v3:
time: 56.1 us; the launch traced here: 55.9 us
  Pallas kernels  39 us (70%)
  blocking collectives  15.5 us (28%)
  between operations  0.79 us (1%)
  local copies, waits for them, and re-layouts  0.66 us (1%)
    pallas_call x1, Pallas kernels, factor(): pl.pallas_call(chol_kernel, out_shape=(jax.ShapeDtypeStruct((1, n, part),...  26.8 us
    all_to_all x1, blocking collectives, per_device(): lax.all_to_all(tiles, ('row', 'col'), split_axis=0, concat_axis=0, tiled=...  15.5 us
    pallas_call x1, Pallas kernels, cross(): pl.pallas_call(functools.partial(cross_kernel, rank), out_shape=(jax.Shap...  10.6 us
    pallas_call x1, Pallas kernels, pack(): pl.pallas_call(functools.partial(pack_kernel, size), out_shape=jax.ShapeD...  1.55 us

profile of v3, /device:TPU:0, one launch (start us, length us, event | category | flops | bytes accessed | tf_op | source)
XLA Modules:
  0.0 55.9 jit_solution(3837049107637687650)
XLA Ops:
  0.6 1.6 %pack.1 = f32[32,8,128]{2,1,0:T(8,128)} custom-call(s32[1,2]{1,0:T(1,128)} %far_ref.3, f32[3,128]{1,0:T(4,128)} %points_ref.1, f32[1,128]{1,0:T(1,128)} %bitcast.1, s32[1,2,2,64]{3,2,1,0:T(2,128)} %row_ref.1, s32[1,2,2,64]{3,2,1,0:T(2,128)} %col_ref.1), custom_call_target="tpu_custom_call" | custom-call | tf_op jit(solution)/shard_map/pack/pallas_call | solution.py:511
  2.2 15.5 %all_to_all.5.tile_ref = f32[32,8,128]{2,1,0:T(8,128)S(1)} all-to-all(f32[32,8,128]{2,1,0:T(8,128)} %pack.1), channel_id=1, replica_groups=mesh['row'=8,'col'=4] {'row','col'}, dimensions={0} | all-to-all | bytes 262144 | tf_op jit(solution)/shard_map/all_to_all | solution.py:526
  17.7 0.0 copy-start
  17.7 0.7 %copy-done = s32[1,2]{1,0:T(1,128)S(1)} copy-done((s32[1,2]{1,0:T(1,128)S(1)}, s32[1,2]{1,0:T(1,128)}, u32[]{:S(2)}) %copy-start) | copy-done | bytes 32
  18.4 10.6 %cross.1 = (bf16[1024,512]{1,0:T(8,128)(2,1)S(1)}, bf16[1,256,512]{2,1,0:T(8,128)(2,1)}) custom-call(s32[1,2]{1,0:T(1,128)S(1)} %copy-done, f32[32,8,128]{2,1,0:T(8,128)S(1)} %all_to_all.5.tile_ref), custom_call_target="tpu_custom_call" | custom-call | tf_op jit(solution)/shard_map/cross/pallas_call | solution.py:477
  29.0 26.8 %factor.1 = (bf16[1,1024,128]{2,1,0:T(8,128)(2,1)}, f32[1,1024,1024]{2,1,0:T(8,128)}) custom-call(bf16[1024,512]{1,0:T(8,128)(2,1)S(1)} %get-tuple-element.8.ucat_ref), custom_call_target="tpu_custom_call" | custom-call | tf_op jit(solution)/shard_map/factor/pallas_call | solution.py:271
Async XLA Ops:
  17.7 0.7 %copy-start = (s32[1,2]{1,0:T(1,128)S(1)}, s32[1,2]{1,0:T(1,128)}, u32[]{:S(2)}) copy-start(s32[1,2]{1,0:T(1,128)} %far_ref.3) | copy-start | bytes 28

commit v4 on v3

--- a/solution.py
+++ b/solution.py
@@ -38,7 +38,7 @@
     return jnp.broadcast_to(x[j : j + 1, :], x.shape)
 
 
-def eliminate(many, groups, near, width=LANES, zero=None, between=None):
+def eliminate(many, groups, near, width=LANES, zero=None):
     shape = many[0][0].shape
     sub = lax.broadcasted_iota(jnp.int32, shape, 0)
     lane = lax.broadcasted_iota(jnp.int32, shape, 1)
@@ -96,9 +96,9 @@
                     mats[g + 1] = mats[g + 1] - c * row
             mats[g] = mats[g] * scale
             if last < groups:
-                inside = (lane >= SUB * g) & (lane < SUB * (g + 1))
+                inside = (spot >= SUB * g) & (spot < SUB * (g + 1))
                 high, low = split(mats[g])
-                right = jnp.where(inside & (lane > SUB * g + sub), 0.0, mats[g])
+                right = jnp.where(inside & (spot > SUB * g + sub), 0.0, mats[g])
                 right_high, right_low = split(right)
                 none = jnp.zeros_like(high)
                 product = dot(
@@ -107,15 +107,17 @@
                     TN,
                 )
                 for i in range(last, groups):
-                    mats[i] = jnp.where(inside, 0.0, mats[i]) - product[SUB * i : SUB * (i + 1), :]
+                    part = product[SUB * i : SUB * (i + 1), :]
+                    for at in range(width, LANES, width):
+                        part = jnp.where(lane < at, part, product[at + SUB * i : at + SUB * (i + 1), :])
+                    mats[i] = jnp.where(inside, 0.0, mats[i]) - part
             for i in range(g + 2 if look else g + 1, last):
                 for j in range(SUB):
                     for t in range(j + 1, SUB):
                         panel[i, t] = panel[i, t] - panel[i, j] * heads[j][t]
                     mats[i] = mats[i] - panel[i, j] * rows[j]
             diagonals[which] = ahead
-        if between:
-            between(g)
+        yield g
 
 
 def factors_of(mats, width=LANES):
@@ -155,7 +157,7 @@
     return out[:, :n] + out[:, n:]
 
 
-def chol_kernel(ucat_ref, basis_ref, tri_ref, a_ref, o_ref, y_ref, d_ref, l_ref, x_ref, p_ref, sems):
+def basis_of(beside, ucat_ref, basis_ref, tri_ref, a_ref, o_ref, y_ref, d_ref, l_ref, x_ref, p_ref, sems):
     n, inner = ucat_ref.shape
     blk = LANES
     nb = n // blk
@@ -180,11 +182,9 @@
         mats = [d[SUB * i : SUB * (i + 1), :] for i in range(groups)]
         turns = steps
 
-        def between(g):
+        for g in eliminate([mats], groups, NEAR, LANES, zero):
             for step in turns[g]:
                 step()
-
-        eliminate([mats], groups, NEAR, LANES, zero, between)
         both, inverse = factors_of(mats)
         return jnp.where(row_id <= col_id, both, 0.0).T, split(inverse)
 
@@ -192,8 +192,10 @@
         nxt = jnp.minimum(b + 1, nb - 1)
         under = pl.ds(pl.multiple_of(nxt * blk, blk), blk)
         here = pl.ds(pl.multiple_of(b * blk, blk), blk)
-        below = split(times_t(pair(a_ref[under, here]), xs))
-        d_ref[...] = a_ref[under, under] - times_t(jnp.concatenate(below, 1), below)
+        strip = a_ref[under, here]
+        below = pair(times_t(pair(strip), xs))
+        across = split(times_t(jnp.concatenate(xs, 1), split(strip)))
+        d_ref[...] = a_ref[under, under] - times(below, across)
         l_ref[...] = low
         x_ref[0] = xs[0]
         x_ref[1] = xs[1]
@@ -211,7 +213,12 @@
         a_ref[rows, cols] = gram(rows, cols)
 
     corner = slice(0, blk)
-    low, xs = diagonal(gram(corner, corner), in_turns([functools.partial(gram_step, *t) for t in tiles], groups))
+    turns = in_turns([functools.partial(gram_step, *t) for t in tiles], groups)
+    for turn in turns:
+        turn.append(lambda: next(beside, None))
+    low, xs = diagonal(gram(corner, corner), turns)
+    for _ in beside:
+        pass
     spread(low, xs, 0)
 
     def block(b, carry):
@@ -263,32 +270,6 @@
     basis_ref[0, last, :] = times(xs, split(y_ref[last, :])).astype(bf16)
     for b in range(nb):
         copy_out(b).wait()
-
-
-def factor(ucat, part):
-    n, inner = ucat.shape
-    vmem = pl.BlockSpec(memory_space=pltpu.VMEM)
-    return pl.pallas_call(
-        chol_kernel,
-        out_shape=(
-            jax.ShapeDtypeStruct((1, n, part), bf16),
-            jax.ShapeDtypeStruct((1, n, n), f32),
-        ),
-        in_specs=[vmem],
-        out_specs=(vmem, pl.BlockSpec(memory_space=pl.ANY)),
-        scratch_shapes=[
-            pltpu.VMEM((n, n), f32),
-            pltpu.VMEM((n // LANES, n, LANES), f32),
-            pltpu.VMEM((n, part), f32),
-            pltpu.VMEM((LANES, LANES), f32),
-            pltpu.VMEM((LANES, LANES), f32),
-            pltpu.VMEM((2, LANES, LANES), bf16),
-            pltpu.VMEM((n, 2 * LANES), bf16),
-            pltpu.SemaphoreType.DMA((n // LANES,)),
-        ],
-        compiler_params=pltpu.CompilerParams(vmem_limit_bytes=48 << 20),
-        name="factor",
-    )(ucat)
 
 
 def wave(a, b):
@@ -309,7 +290,7 @@
     return jnp.concatenate([jnp.where(left, x, none), jnp.where(left, none, x)], 0)
 
 
-def shifted_inverse(tops, look, fillers):
+def shifted_normals(tops):
     rank = tops[0].shape[0]
     groups = rank // SUB
     r = lax.broadcasted_iota(jnp.int32, tops[0].shape, 0)
@@ -324,18 +305,10 @@
         shift = jnp.where(first, shift[0], shift[1]) * (1.0 / rank) + 1e-06
         normal = normal + jnp.where(r == c % rank, shift, 0.0)
         mats.append([normal[SUB * i : SUB * (i + 1), :] for i in range(groups)])
-    zero = jnp.zeros((SUB, LANES), f32) + jnp.max(tops[0]) * 0.0 if look else None
-    turns = in_turns(fillers, groups)
-
-    def between(g):
-        for step in turns[g]:
-            step()
-
-    eliminate(mats, groups, groups, rank, zero, between)
-    return [factors_of(rows, rank)[1] for rows in mats]
-
-
-def cross_kernel(rank, far_ref, tile_ref, ucat_ref, right_ref, pts_ref, ij_ref, ijt_ref, low_ref, half_ref, v_ref, panel_ref):
+    return mats
+
+
+def cross_blocks(rank, far_ref, tile_ref, ucat_ref, right_ref, pts_ref, ij_ref, ijt_ref, low_ref, half_ref, v_ref, panel_ref):
     devices = tile_ref.shape[0]
     cols = lax.axis_size("col")
     clusters = devices // cols
@@ -431,7 +404,13 @@
         fillers += [
             functools.partial(row_panel, s, k, h, i_col[k][h], there[h]) for k in range(2) for h in range(2)
         ]
-    lowers = shifted_inverse([p[1] for p in pairs], False, fillers)
+    groups = rank // SUB
+    normals = shifted_normals([p[1] for p in pairs])
+    turns = in_turns(fillers, groups)
+    for g in eliminate(normals, groups, groups, rank):
+        for step in turns[g]:
+            step()
+    lowers = [factors_of(rows, rank)[1] for rows in normals]
     for (s, top, mixed, _), low in zip(pairs, lowers):
         half = times(pair(low), split(apart(top, left)))
         low_ref[s // 2] = low
@@ -439,6 +418,9 @@
         v_t = times_t(pair(mixed), split(apart(half, left)))
         v_ref[s // 2] = times(pair(v_t), split(apart(low, left))).astype(bf16)
 
+    for p in pairs:
+        next_left_factor(p[0], p[3])
+
     square = lax.broadcasted_iota(jnp.int32, (LANES, LANES), 0) < rank
     same = square == (lax.broadcasted_iota(jnp.int32, (LANES, LANES), 1) < rank)
 
@@ -449,40 +431,51 @@
         both = jnp.concatenate([high, low], 1)
         return dot(both, jnp.concatenate([panel_high, panel_high], 0), NN) + dot(high, panel_low, NN)
 
-    fillers = [functools.partial(next_left_factor, p[0], p[3]) for p in pairs]
     for s, which, i_col, j_col, j_row, i_row, there in mine:
         top = wave(both_columns(*j_col[1]), i_row)
         u_i = wave(both_columns(*j_col[0]), i_row).astype(bf16)
         top = top - dot(v_ref[which], apart(u_i, left), NN)
+        normals = shifted_normals([top])
         v0 = couple(low_ref[which], half_ref[which], panel_ref[s // 2, 0]).astype(bf16)
         u_t = wave(both_columns(*i_col[1]), j_row).astype(bf16)
         rest = panel_ref[s // 2, 1] - dot(apart(u_t, left), v0, NN)
-        low = shifted_inverse([top], True, fillers[:len(pairs) - 1])[0]
-        fillers = fillers[len(pairs) - 1:]
-        v1 = couple(low, times(pair(low), split(apart(top, left))), rest).astype(bf16)
+        zero = jnp.zeros((SUB, LANES), f32) + jnp.max(top) * 0.0
+        yield from eliminate(normals, groups, groups, rank, zero)
+        low = factors_of(normals[0], rank)[1]
+        half = times(pair(low), split(apart(top, left)))
+        yield groups
+        v1 = couple(low, half, rest).astype(bf16)
         for h in range(2):
             at = (s + h) * 2 * rank
             right_ref[0, at : at + rank, :] = v0[h * rank : (h + 1) * rank]
             right_ref[0, at + rank : at + 2 * rank, :] = v1[h * rank : (h + 1) * rank]
-    for step in fillers:
-        step()
-
-
-def cross(far_blocks, tiles, rank, cols):
+        yield groups + 1
+
+
+def main_kernel(rank, far_ref, tile_ref, right_ref, basis_ref, tri_ref, ucat_ref, *scratch):
+    beside = cross_blocks(rank, far_ref, tile_ref, ucat_ref, right_ref, *scratch[:7])
+    next(beside)
+    basis_of(beside, ucat_ref, basis_ref, tri_ref, *scratch[7:])
+
+
+def blocks_and_basis(far_blocks, tiles, rank, cols):
     local = far_blocks.shape[1]
     slots = cols * local
     clusters = tiles.shape[0] // cols
     size = cols * LANES
+    n = slots * 2 * rank
     vmem = pl.BlockSpec(memory_space=pltpu.VMEM)
     return pl.pallas_call(
-        functools.partial(cross_kernel, rank),
+        functools.partial(main_kernel, rank),
         out_shape=(
-            jax.ShapeDtypeStruct((slots * 2 * rank, size), bf16),
             jax.ShapeDtypeStruct((1, local * 2 * rank, size), bf16),
+            jax.ShapeDtypeStruct((1, n, LANES), bf16),
+            jax.ShapeDtypeStruct((1, n, n), f32),
         ),
         in_specs=[pl.BlockSpec(memory_space=pltpu.SMEM), vmem],
-        out_specs=(vmem, vmem),
+        out_specs=(vmem, vmem, pl.BlockSpec(memory_space=pl.ANY)),
         scratch_shapes=[
+            pltpu.VMEM((n, size), bf16),
             pltpu.VMEM((16 * clusters, size), bf16),
             pltpu.VMEM((8 * slots, LANES), f32),
             pltpu.VMEM((LANES, LANES), f32),
@@ -490,9 +483,17 @@
             pltpu.VMEM((slots // 2, rank, LANES), f32),
             pltpu.VMEM((slots // 2, rank, LANES), bf16),
             pltpu.VMEM((local // 2, 2, 2 * rank, size), f32),
+            pltpu.VMEM((n, n), f32),
+            pltpu.VMEM((n // LANES, n, LANES), f32),
+            pltpu.VMEM((n, LANES), f32),
+            pltpu.VMEM((LANES, LANES), f32),
+            pltpu.VMEM((LANES, LANES), f32),
+            pltpu.VMEM((2, LANES, LANES), bf16),
+            pltpu.VMEM((n, 2 * LANES), bf16),
+            pltpu.SemaphoreType.DMA((n // LANES,)),
         ],
         compiler_params=pltpu.CompilerParams(vmem_limit_bytes=48 << 20),
-        name="cross",
+        name="blocks_and_basis",
     )(far_blocks, tiles)
 
 
@@ -524,8 +525,7 @@
     count = lax.axis_size("row") * cols
     tiles = pack(far_blocks, points, weights, row_pivots, col_pivots, count, part * cols)
     tiles = lax.all_to_all(tiles, ("row", "col"), split_axis=0, concat_axis=0, tiled=True)
-    ucat, factors_v = cross(far_blocks, tiles, rank, cols)
-    basis, lower = factor(ucat, part)
+    factors_v, basis, lower = blocks_and_basis(far_blocks, tiles, rank, cols)
     return factors_v, basis, lower
 
 

time: 56.1 us -> 54.6 us (0.973)
  Pallas kernels: 39 us -> 37.4 us
    pallas_call x2 -> x1, Pallas kernels: 37.4 us -> 35.8 us  [blocks_and_basis(): pl.pallas_call(functools.partial(main_kernel, rank), out_shape=(jax.Shape...]
where the time goes in v4:
time: 54.6 us; the launch traced here: 54.4 us
  Pallas kernels  37.4 us (68%)
  blocking collectives  15.5 us (28%)
  between operations  0.79 us (1%)
  local copies, waits for them, and re-layouts  0.66 us (1%)
    pallas_call x1, Pallas kernels, blocks_and_basis(): pl.pallas_call(functools.partial(main_kernel, rank), out_shape=(jax.Shape...  35.8 us
    all_to_all x1, blocking collectives, per_device(): lax.all_to_all(tiles, ('row', 'col'), split_axis=0, concat_axis=0, tiled=...  15.5 us
    pallas_call x1, Pallas kernels, pack(): pl.pallas_call(functools.partial(pack_kernel, size), out_shape=jax.ShapeD...  1.55 us

profile of v4, /device:TPU:0, one launch (start us, length us, event | category | flops | bytes accessed | tf_op | source)
XLA Modules:
  0.0 54.4 jit_solution(14941841367967054174)
XLA Ops:
  0.6 1.6 %pack.1 = f32[32,8,128]{2,1,0:T(8,128)} custom-call(s32[1,2]{1,0:T(1,128)} %far_ref.3, f32[3,128]{1,0:T(4,128)} %points_ref.1, f32[1,128]{1,0:T(1,128)} %bitcast.1, s32[1,2,2,64]{3,2,1,0:T(2,128)} %row_ref.1, s32[1,2,2,64]{3,2,1,0:T(2,128)} %col_ref.1), custom_call_target="tpu_custom_call" | custom-call | tf_op jit(solution)/shard_map/pack/pallas_call | solution.py:512
  2.2 15.5 %all_to_all.5.tile_ref = f32[32,8,128]{2,1,0:T(8,128)S(1)} all-to-all(f32[32,8,128]{2,1,0:T(8,128)} %pack.1), channel_id=1, replica_groups=mesh['row'=8,'col'=4] {'row','col'}, dimensions={0} | all-to-all | bytes 262144 | tf_op jit(solution)/shard_map/all_to_all | solution.py:527
  17.7 0.0 copy-start
  17.7 0.7 %copy-done = s32[1,2]{1,0:T(1,128)S(1)} copy-done((s32[1,2]{1,0:T(1,128)S(1)}, s32[1,2]{1,0:T(1,128)}, u32[]{:S(2)}) %copy-start) | copy-done | bytes 32
  18.4 35.8 %blocks_and_basis.1 = (bf16[1,256,512]{2,1,0:T(8,128)(2,1)}, bf16[1,1024,128]{2,1,0:T(8,128)(2,1)}, f32[1,1024,1024]{2,1,0:T(8,128)}) custom-call(s32[1,2]{1,0:T(1,128)S(1)} %copy-done, f32[32,8,128]{2,1,0:T(8,128)S(1)} %all_to_all.5.tile_ref), custom_call_target="tpu_custom_call" | custom-call | tf_op jit(solution)/shard_map/blocks_and_basis/pallas_call | solution.py:468
Async XLA Ops:
  17.7 0.7 %copy-start = (s32[1,2]{1,0:T(1,128)S(1)}, s32[1,2]{1,0:T(1,128)}, u32[]{:S(2)}) copy-start(s32[1,2]{1,0:T(1,128)} %far_ref.3) | copy-start | bytes 28

commit v5 on v4

--- a/solution.py
+++ b/solution.py
@@ -334,8 +334,11 @@
                 panel = tile_ref[row * cols + c, 4 + kind * local + s : 5 + kind * local + s, :].astype(jnp.int32)
                 where = panel // size
                 hot = jnp.where(spots == panel - where * size, 1.0, 0.0).astype(bf16)
-                got = dot(pts_ref[...], hot, NN).reshape(clusters, 16, LANES)
-                got = jnp.sum(jnp.where(of == where[None], got, 0.0), axis=0)
+                if kind == 0:
+                    got = dot(pts_ref[pl.ds(pl.multiple_of(16 * row, 16), 16), :], hot, NN)
+                else:
+                    got = dot(pts_ref[...], hot, NN).reshape(clusters, 16, LANES)
+                    got = jnp.sum(jnp.where(of == where[None], got, 0.0), axis=0)
                 found.append(got[0:4] + got[4:8] + got[8:12])
             at = 8 * (c * local + s)
             ij_ref[at : at + 8, :] = jnp.concatenate(found, 0)

time: 54.6 us -> 54.3 us (level)
  no operation moved by 1% of the time
where the time goes in v5:
time: 54.3 us; the launch traced here: 54.1 us
  Pallas kernels  37.1 us (68%)
  blocking collectives  15.5 us (29%)
  between operations  0.79 us (1%)
  local copies, waits for them, and re-layouts  0.66 us (1%)
    pallas_call x1, Pallas kernels, blocks_and_basis(): pl.pallas_call(functools.partial(main_kernel, rank), out_shape=(jax.Shape...  35.6 us
    all_to_all x1, blocking collectives, per_device(): lax.all_to_all(tiles, ('row', 'col'), split_axis=0, concat_axis=0, tiled=...  15.5 us
    pallas_call x1, Pallas kernels, pack(): pl.pallas_call(functools.partial(pack_kernel, size), out_shape=jax.ShapeD...  1.55 us

profile of v5, /device:TPU:0, one launch (start us, length us, event | category | flops | bytes accessed | tf_op | source)
XLA Modules:
  0.0 54.1 jit_solution(6528202581704593492)
XLA Ops:
  0.6 1.6 %pack.1 = f32[32,8,128]{2,1,0:T(8,128)} custom-call(s32[1,2]{1,0:T(1,128)} %far_ref.3, f32[3,128]{1,0:T(4,128)} %points_ref.1, f32[1,128]{1,0:T(1,128)} %bitcast.1, s32[1,2,2,64]{3,2,1,0:T(2,128)} %row_ref.1, s32[1,2,2,64]{3,2,1,0:T(2,128)} %col_ref.1), custom_call_target="tpu_custom_call" | custom-call | tf_op jit(solution)/shard_map/pack/pallas_call | solution.py:515
  2.2 15.5 %all_to_all.5.tile_ref = f32[32,8,128]{2,1,0:T(8,128)S(1)} all-to-all(f32[32,8,128]{2,1,0:T(8,128)} %pack.1), channel_id=1, replica_groups=mesh['row'=8,'col'=4] {'row','col'}, dimensions={0} | all-to-all | bytes 262144 | tf_op jit(solution)/shard_map/all_to_all | solution.py:530
  17.7 0.0 copy-start
  17.7 0.7 %copy-done = s32[1,2]{1,0:T(1,128)S(1)} copy-done((s32[1,2]{1,0:T(1,128)S(1)}, s32[1,2]{1,0:T(1,128)}, u32[]{:S(2)}) %copy-start) | copy-done | bytes 32
  18.4 35.6 %blocks_and_basis.1 = (bf16[1,256,512]{2,1,0:T(8,128)(2,1)}, bf16[1,1024,128]{2,1,0:T(8,128)(2,1)}, f32[1,1024,1024]{2,1,0:T(8,128)}) custom-call(s32[1,2]{1,0:T(1,128)S(1)} %copy-done, f32[32,8,128]{2,1,0:T(8,128)S(1)} %all_to_all.5.tile_ref), custom_call_target="tpu_custom_call" | custom-call | tf_op jit(solution)/shard_map/blocks_and_basis/pallas_call | solution.py:471
Async XLA Ops:
  17.7 0.7 %copy-start = (s32[1,2]{1,0:T(1,128)S(1)}, s32[1,2]{1,0:T(1,128)}, u32[]{:S(2)}) copy-start(s32[1,2]{1,0:T(1,128)} %far_ref.3) | copy-start | bytes 28
